TPU v7x, 32 devices: a whole 2x2x4 slice. The times are simulated.
32 devices in a mesh: cfg: 2 (over y), ta: 2 (over x), gz: 4 (over z), gy: 2 (over core).
Axes of the slice: x: 2, y: 2, z: 4, core: 2. Of those that a mesh axis runs over, the one named last changes fastest.
Arguments:
- spatial_links: float32 [6, 2, 3, 3, 4, 4, 16, 128], P('cfg', None, None, None, 'ta', 'gz', 'gy'), parts along dimension 0, may hold values from -1 to 1
- time_links: float32 [4, 3, 3, 4, 4, 16, 128], P('cfg', None, None, 'ta', 'gz', 'gy'), parts along dimension 0, may hold values from -1 to 1
Outputs:
- polyakov: float32 [4, 4, 16, 128], P('cfg', 'gz', 'gy'), parts along dimension 0
- site_mean: float32 [4], P('cfg'), parts along dimension 0
There are 2 independent parts, one for each index of `cfg`. A program takes and returns all parts, laid end to end along the dimension named above; each array names one. Nothing has to cross between parts.
All inputs are finite; a program needn't handle non-finite values.
Results may differ from a plain program's by a relative error of at most 0.0003.
Values sent between devices are 32-bit elements; how exact they have to be, the bound alone decides.
A program may use at most 64 MiB of HBM per device.

v0:
```python
from functools import partial

import jax
import jax.numpy as jnp
from jax import lax
from jax.experimental import pallas as pl
from jax.experimental.pallas import tpu as pltpu
from jax.sharding import PartitionSpec as P

ITERS = 3


smear_weight = 0.5
norm_floor = 0.25
unit_steps = ((1, 0, 0), (0, 1, 0), (0, 0, 1))


def padded_2(cells, sides, width):
    for axis, dim in sides:
        count = lax.axis_size(axis)
        head = lax.slice_in_dim(cells, 0, width, axis=dim)
        tail = lax.slice_in_dim(cells, cells.shape[dim] - width, cells.shape[dim], axis=dim)
        cells = jnp.concatenate(
            [
                lax.ppermute(tail, axis, [(i, (i + 1) % count) for i in range(count)]),
                cells,
                lax.ppermute(head, axis, [((i + 1) % count, i) for i in range(count)]),
            ],
            axis=dim,
        )
    return cells


def shifted(shard, axis, by):
    devices = lax.axis_size(axis)
    return lax.ppermute(shard, axis, [(i, (i + by) % devices) for i in range(devices)])


def mat_product(lhs_mat, rhs_mat):
    lhs_re = lhs_mat[0][:, :, None]
    lhs_im = lhs_mat[1][:, :, None]
    rhs_re = rhs_mat[0][None]
    rhs_im = rhs_mat[1][None]
    real_part = jnp.sum(lhs_re * rhs_re - lhs_im * rhs_im, axis=1)
    imag_part = jnp.sum(lhs_re * rhs_im + lhs_im * rhs_re, axis=1)
    return jnp.stack([real_part, imag_part])


def dagger(matrix):
    return jnp.stack([jnp.swapaxes(matrix[0], 0, 1), -jnp.swapaxes(matrix[1], 0, 1)])


def normalize_row(row_vec):
    weight = jnp.sum(row_vec[0] * row_vec[0] + row_vec[1] * row_vec[1], axis=0)
    return row_vec / jnp.sqrt(jnp.maximum(weight, norm_floor))


def project(matrix):
    first = normalize_row(matrix[:, 0])
    second_raw = matrix[:, 1]
    inner_re = jnp.sum(first[0] * second_raw[0] + first[1] * second_raw[1], axis=0)
    inner_im = jnp.sum(first[0] * second_raw[1] - first[1] * second_raw[0], axis=0)
    ortho = jnp.stack(
        [
            second_raw[0] - (inner_re * first[0] - inner_im * first[1]),
            second_raw[1] - (inner_re * first[1] + inner_im * first[0]),
        ]
    )
    second = normalize_row(ortho)
    first_one = jnp.roll(first, -1, axis=1)
    first_two = jnp.roll(first, -2, axis=1)
    second_one = jnp.roll(second, -1, axis=1)
    second_two = jnp.roll(second, -2, axis=1)
    cross_re = (
        first_one[0] * second_two[0]
        - first_one[1] * second_two[1]
        - (first_two[0] * second_one[0] - first_two[1] * second_one[1])
    )
    cross_im = (
        first_one[0] * second_two[1]
        + first_one[1] * second_two[0]
        - (first_two[0] * second_one[1] + first_two[1] * second_one[0])
    )
    third = jnp.stack([cross_re, -cross_im])
    return jnp.stack([first, second, third], axis=1)


def moved(offset, unit_vec, factor):
    return (
        offset[0] + factor * unit_vec[0],
        offset[1] + factor * unit_vec[1],
        offset[2] + factor * unit_vec[2],
    )


def smear_spatial(neighbour):
    anchor = (0, 0, 0)
    result = []
    for mu_dir in range(3):
        staples = None
        for nu_dir in range(3):
            if nu_dir == mu_dir:
                continue
            forward = unit_steps[nu_dir]
            sideways = unit_steps[mu_dir]
            upper_staple = mat_product(
                mat_product(neighbour(nu_dir, anchor), neighbour(mu_dir, forward)),
                dagger(neighbour(nu_dir, sideways)),
            )
            back_offset = moved(anchor, forward, -1)
            lower_staple = mat_product(
                mat_product(dagger(neighbour(nu_dir, back_offset)), neighbour(mu_dir, back_offset)),
                neighbour(nu_dir, moved(back_offset, sideways, 1)),
            )
            if staples is None:
                staples = upper_staple + lower_staple
            else:
                staples = staples + upper_staple + lower_staple
        mixed_link = (1.0 - smear_weight) * neighbour(mu_dir, anchor) + smear_weight / 4.0 * staples
        result.append(project(mixed_link))
    return jnp.stack(result)


def window_cut(field, offset):
    z_inner = field.shape[-3] - 2
    y_inner = field.shape[-2] - 2
    piece = field[
        ..., 1 + offset[2] : 1 + offset[2] + z_inner, 1 + offset[1] : 1 + offset[1] + y_inner, :
    ]
    return jnp.roll(piece, -offset[0], axis=-1)


def padded_neighbour(padded, direction, offset):
    return window_cut(padded[direction], offset)


def smooth_by_products(link_field, time_links, extended, depth):
    later_links = extended[0:3, :, :, :, 1 : depth + 1]
    lowers = [
        mat_product(mat_product(dagger(link_field[nu_dir]), time_links), later_links[nu_dir])
        for nu_dir in range(3)
    ]
    carried = jnp.stack([time_links] + lowers)
    padded = padded_2(carried, (("gz", 5), ("gy", 6)), 1)
    anchor = (0, 0, 0)
    staples = None
    for nu_dir in range(3):
        forward = unit_steps[nu_dir]
        upper_staple = mat_product(
            mat_product(link_field[nu_dir], window_cut(padded[0], forward)),
            dagger(later_links[nu_dir]),
        )
        lower_staple = window_cut(padded[1 + nu_dir], moved(anchor, forward, -1))
        if staples is None:
            staples = upper_staple + lower_staple
        else:
            staples = staples + upper_staple + lower_staple
    mixed_link = (1.0 - smear_weight) * time_links + smear_weight / 6.0 * staples
    return project(mixed_link)


def on_device(spatial_links, time_links):
    link_field = spatial_links
    for sweep_index in range(ITERS):
        padded = padded_2(link_field, (("gz", 5), ("gy", 6)), 1)
        link_field = smear_spatial(partial(padded_neighbour, padded))
    stacked = jnp.concatenate([link_field, time_links[None]], axis=0)
    ahead_slice = shifted(stacked[:, :, :, :, 0:1], "ta", -1)
    extended = jnp.concatenate([stacked, ahead_slice], axis=4)
    depth = time_links.shape[3]
    smoothed = smooth_by_products(link_field, time_links, extended, depth)
    block_prod = smoothed[:, :, :, 0]
    block_prod = mat_product(block_prod, smoothed[:, :, :, 1])
    pieces = lax.all_gather(block_prod[None], "ta", axis=0, tiled=True)

    def advance(index, carry):
        return mat_product(carry, pieces[index])

    whole_prod = lax.fori_loop(1, pieces.shape[0], advance, pieces[0])
    polyakov = (
        jnp.stack(
            [
                whole_prod[0, 0, 0] + whole_prod[0, 1, 1] + whole_prod[0, 2, 2],
                whole_prod[1, 0, 0] + whole_prod[1, 1, 1] + whole_prod[1, 2, 2],
            ]
        )
        / 3.0
    )
    local_sums = jnp.sum(polyakov, axis=(1, 2, 3))
    totals = lax.psum(local_sums, ("gz", "gy"))
    site_count = (
        polyakov.shape[1]
        * polyakov.shape[2]
        * polyakov.shape[3]
        * lax.axis_size("gz")
        * lax.axis_size("gy")
    )
    site_mean = totals / site_count
    return (polyakov, site_mean)


HALO = ITERS + 1
MESH_ID = pl.DeviceIdType.MESH


def signed_sum(terms):
    total = None
    for sign, value in terms:
        if total is None:
            total = value if sign > 0 else -value
        elif sign > 0:
            total = total + value
        else:
            total = total - value
    return total


def times(lhs, rhs, lhs_dag=False, rhs_dag=False, rows=3):
    out = []
    for i in range(rows):
        line = []
        for j in range(3):
            real_terms, imag_terms = [], []
            for k in range(3):
                a_re, a_im = lhs[k][i] if lhs_dag else lhs[i][k]
                b_re, b_im = rhs[j][k] if rhs_dag else rhs[k][j]
                sa = -1 if lhs_dag else 1
                sb = -1 if rhs_dag else 1
                real_terms += [(1, a_re * b_re), (-sa * sb, a_im * b_im)]
                if sb > 0:
                    imag_terms += [(1, a_re * b_im), (sa, a_im * b_re)]
                else:
                    imag_terms += [(1, a_im * b_re), (-1, a_re * b_im)]
            line.append((signed_sum(real_terms), signed_sum(imag_terms)))
        out.append(line)
    return out


def unit_row(row):
    weight = signed_sum([(1, p * p) for pair in row for p in pair])
    scale = lax.rsqrt(jnp.maximum(weight, norm_floor))
    return [(re * scale, im * scale) for re, im in row]


def third_row(first, second):
    out = []
    for j in range(3):
        (a_re, a_im), (b_re, b_im) = first[(j + 1) % 3], second[(j + 2) % 3]
        (c_re, c_im), (d_re, d_im) = first[(j + 2) % 3], second[(j + 1) % 3]
        re = a_re * b_re - a_im * b_im - (c_re * d_re - c_im * d_im)
        im = c_re * d_im + c_im * d_re - (a_re * b_im + a_im * b_re)
        out.append((re, im))
    return out


def project_rows(rows):
    first = unit_row(rows[0])
    inner_re = signed_sum(
        [(1, p) for (a, b), (c, d) in zip(first, rows[1]) for p in (a * c, b * d)]
    )
    inner_im = None
    for (a, b), (c, d) in zip(first, rows[1]):
        part = a * d - b * c
        inner_im = part if inner_im is None else inner_im + part
    ortho = [
        (c - (inner_re * a - inner_im * b), d - (inner_re * b + inner_im * a))
        for (a, b), (c, d) in zip(first, rows[1])
    ]
    second = unit_row(ortho)
    return [first, second, third_row(first, second)]


def fused_kernel(
    dims, sl_hbm, tl_hbm, poly_ref, mean_ref,
    raw, packed, landed, state, ups, lows, outgoing, ahead, smooth_out, smooth_in,
    trace_out, traces, row_out, rows_in,
    load_sem, a_send, a_recv, n_send, n_recv, w_send, w_recv,
    t_send, t_recv, r_send, r_recv,
):
    n_ta, n_gz, n_gy, width, sites = dims
    quarter = width // n_gz
    window = quarter + 2 * HALO
    seg = width // 2
    a, k, c = lax.axis_index("ta"), lax.axis_index("gz"), lax.axis_index("gy")
    lane = lax.broadcasted_iota(jnp.int32, (8, width), 1)
    row_id = lax.broadcasted_iota(jnp.int32, (8, width), 0)
    n_group = n_ta * n_gz * n_gy
    my_rank = (a * n_gz + k) * n_gy + c

    loads = [pltpu.make_async_copy(sl_hbm.at[d], raw.at[d], load_sem.at[d]) for d in range(3)]
    loads.append(pltpu.make_async_copy(tl_hbm, raw.at[3], load_sem.at[3]))
    for copy in loads:
        copy.start()

    def peer(step):
        rank = lax.rem(my_rank + step, n_group)
        return {
            "ta": rank // (n_gz * n_gy),
            "gz": lax.rem(rank // n_gy, n_gz),
            "gy": lax.rem(rank, n_gy),
        }

    barrier = pltpu.get_barrier_semaphore()
    for step in range(1, n_group):
        pl.semaphore_signal(barrier, inc=1, device_id=peer(step), device_id_type=MESH_ID)

    wide = lax.broadcasted_iota(jnp.int32, (32, width), 1)

    def side_by_side(blocks, shift_of):
        tile = None
        for j in range(3):
            moved_block = pltpu.roll(blocks[j].reshape(32, width), shift_of(j), 1)
            tile = moved_block if j == 0 else jnp.where(wide >= window * j, moved_block, tile)
        return tile.reshape(2, 2, 8, width)

    def pack(hop, d):
        dest = lax.rem(k + hop, n_gz)
        for t in range(2):
            blocks = [raw[d, :, 0:2, j, t] for j in range(3)]
            packed[hop, t, d] = side_by_side(
                blocks,
                lambda j: lax.rem(window * j + HALO + width - quarter * dest + width, width),
            )

    groups = ((0, 1), (2,), (3,))

    def exchange(hop, t_rel, group):
        dest = lax.rem(k + hop, n_gz)
        t = lax.rem(c + t_rel, 2)
        part = pl.ds(groups[group][0], len(groups[group]))
        src = packed.at[hop, t, part]
        dst = landed.at[k, c, part]
        if hop == 0 and t_rel == 0:
            return pltpu.make_async_copy(src, dst, a_recv.at[group, k, c])
        return pltpu.make_async_remote_copy(
            src_ref=src, dst_ref=dst,
            send_sem=a_send.at[group, hop, t_rel], recv_sem=a_recv.at[group, k, c],
            device_id={"gz": dest, "gy": t}, device_id_type=MESH_ID,
        )

    hops = [2, 3, 1, 0]
    waited = False
    for group, members in enumerate(groups):
        for d in members:
            loads[d].wait()
        for d in members:
            pack(hops[0], d)
        if not waited:
            pl.semaphore_wait(barrier, n_group - 1)
            waited = True
        for n, hop in enumerate(hops):
            if n + 1 < len(hops):
                for d in members:
                    pack(hops[n + 1], d)
            for t_rel in range(2):
                exchange(hop, t_rel, group).start()

    def arrived(group):
        part = pl.ds(groups[group][0], len(groups[group]))
        for z in range(n_gz):
            for h in range(2):
                ref = landed.at[z, h, part]
                pltpu.make_async_copy(ref, ref, a_recv.at[group, z, h]).wait()

    def spread(read, v, h):
        rows = []
        for r in range(2):
            line = []
            for j in range(3):
                pair = []
                for ri in range(2):
                    low = pltpu.roll(read(v, h, ri, r), (width - window * j) % width, 1)
                    high = pltpu.roll(
                        read(2 + v, h, ri, r), (width + seg - window * j) % width, 1
                    )
                    pair.append(jnp.where(lane < seg, low, high))
                line.append(tuple(pair))
            rows.append(line)
        rows.append(third_row(rows[0], rows[1]))
        return rows

    def unpack(d):
        for v in range(2):
            for h in range(2):
                put(d, v, h, spread(lambda z, hh, ri, r: landed[z, hh, d, ri, r], v, h))

    def put(d, v, h, mat):
        for r in range(3):
            for j in range(3):
                for ri in range(2):
                    state[d, ri, r, j, v, h] = mat[r][j][ri]

    def get(read, rows=3):
        return [[(read(0, r, j), read(1, r, j)) for j in range(3)] for r in range(rows)]

    def shift_plus(read, nu, v, h):
        if nu == 0:
            return pltpu.roll(read(v, h), width - 1, 1)
        if nu == 1:
            return jnp.where(
                row_id == 7, pltpu.roll(read(v, 1 - h), 7, 0), pltpu.roll(read(v, h), 7, 0)
            )
        return pltpu.roll(read(1 - v, h), seg * v, 1)

    def shift_minus(read, nu, v, h):
        if nu == 0:
            return pltpu.roll(read(v, h), 1, 1)
        if nu == 1:
            return jnp.where(
                row_id == 0, pltpu.roll(read(v, 1 - h), 1, 0), pltpu.roll(read(v, h), 1, 0)
            )
        return pltpu.roll(read(1 - v, h), seg * (1 - v), 1)

    def here(d, v, h):
        return get(lambda ri, r, j: state[d, ri, r, j, v, h])

    def plus(d, nu, v, h):
        return get(
            lambda ri, r, j: shift_plus(lambda vv, hh: state[d, ri, r, j, vv, hh], nu, v, h)
        )

    def keep(ref, slot, v, h, mat):
        for r in range(2):
            for j in range(3):
                for ri in range(2):
                    ref[slot, ri, r, j, v, h] = mat[r][j][ri]

    pairs = [(0, 1), (0, 2), (1, 2)]
    slot_of = {}
    for mu in range(3):
        for nu in range(3):
            if mu != nu:
                slot_of[mu, nu] = len(slot_of)

    def staples_at(chosen, index, carry):
        v, h = index // 2, lax.rem(index, 2)
        for mu, nu in chosen:
            u_mu, u_nu = here(mu, v, h), here(nu, v, h)
            nu_ahead, mu_ahead = plus(nu, mu, v, h), plus(mu, nu, v, h)
            one = times(u_mu, nu_ahead)
            keep(lows, slot_of[mu, nu], v, h, times(u_nu, one, lhs_dag=True, rows=2))
            keep(ups, slot_of[nu, mu], v, h, times(one, mu_ahead, rhs_dag=True, rows=2))
            two = times(u_nu, mu_ahead)
            keep(lows, slot_of[nu, mu], v, h, times(u_mu, two, lhs_dag=True, rows=2))
            keep(ups, slot_of[mu, nu], v, h, times(two, nu_ahead, rhs_dag=True, rows=2))
        return carry

    def mix(d, v, h, entries, factor):
        def entry(ri, r, j):
            total = None
            for slot, nu in entries:
                low = shift_minus(lambda vv, hh: lows[slot, ri, r, j, vv, hh], nu, v, h)
                part = ups[slot, ri, r, j, v, h] + low
                total = part if total is None else total + part
            return (1.0 - smear_weight) * state[d, ri, r, j, v, h] + factor * total

        return project_rows(get(entry, rows=2))

    def update_at(chosen, index, carry):
        v, h = index // 2, lax.rem(index, 2)
        for mu in chosen:
            entries = [(slot_of[mu, nu], nu) for nu in range(3) if nu != mu]
            put(mu, v, h, mix(mu, v, h, entries, smear_weight / 4.0))
        return carry

    def staples(chosen):
        lax.fori_loop(0, 4, partial(staples_at, chosen), 0)

    def update(chosen):
        lax.fori_loop(0, 4, partial(update_at, chosen), 0)

    def sweep(index, carry):
        staples(pairs)
        update((0, 1, 2))
        return carry

    arrived(0)
    unpack(0)
    unpack(1)
    staples(pairs[0:1])
    arrived(1)
    unpack(2)
    staples(pairs[1:3])
    update((0, 1, 2))
    lax.fori_loop(0, ITERS - 2, sweep, 0)

    next_copies = [
        pltpu.make_async_remote_copy(
            src_ref=outgoing.at[mu], dst_ref=ahead.at[mu],
            send_sem=n_send.at[mu], recv_sem=n_recv.at[mu],
            device_id={"ta": lax.rem(a + c + n_ta - 1, n_ta), "gy": 1 - c},
            device_id_type=MESH_ID,
        )
        for mu in range(3)
    ]

    def send_next(mu):
        for v in range(2):
            for h in range(2):
                blocks = [state[mu, :, 0:2, j, v, h] for j in range(3)]
                for s in range(2):
                    outgoing[mu, 2 * s + v, h] = side_by_side(
                        blocks, lambda j: (window * j + width - seg * s) % width
                    )
        next_copies[mu].start()

    staples(pairs[0:2])
    update((0,))
    send_next(0)
    staples(pairs[2:3])
    update((1,))
    send_next(1)
    update((2,))
    send_next(2)
    arrived(2)
    unpack(3)

    def time_firsts_at(index, carry):
        v, h = index // 2, lax.rem(index, 2)
        for nu in range(3):
            u_nu = here(nu, v, h)
            keep(ups, nu, v, h, times(u_nu, plus(3, nu, v, h), rows=2))
            keep(lows, nu, v, h, times(u_nu, here(3, v, h), lhs_dag=True, rows=2))
        return carry

    def time_staples_at(nu, index, carry):
        v, h = index // 2, lax.rem(index, 2)
        later = spread(lambda z, hh, ri, r: ahead[nu, z, hh, ri, r], v, h)
        up = get(lambda ri, r, j: ups[nu, ri, r, j, v, h], rows=2)
        keep(ups, nu, v, h, times(up, later, rhs_dag=True, rows=2))
        low = get(lambda ri, r, j: lows[nu, ri, r, j, v, h], rows=2)
        keep(lows, nu, v, h, times(low, later, rows=2))
        return carry

    place = lax.rem(lane, seg)
    inside = (place >= HALO) & (place < HALO + quarter)

    def smooth_at(index, carry):
        v, h = index // 2, lax.rem(index, 2)
        mat = mix(3, v, h, [(nu, nu) for nu in range(3)], smear_weight / 6.0)
        for r in range(2):
            for j in range(3):
                re, im = mat[r][j]
                smooth_out[v, h, r, j] = jnp.where(inside, re, pltpu.roll(im, quarter, 1))
        return carry

    lax.fori_loop(0, 4, time_firsts_at, 0)
    for nu in range(3):
        next_copies[nu].wait_recv()
        lax.fori_loop(0, 4, partial(time_staples_at, nu), 0)
    lax.fori_loop(0, 4, smooth_at, 0)

    w_copies = []
    for da, dc in ((1, 0), (1, 1), (0, 1)):
        to_a, to_c = lax.rem(a + da, n_ta), lax.rem(c + dc, n_gy)
        copy = pltpu.make_async_remote_copy(
            src_ref=smooth_out.at[to_c, to_a], dst_ref=smooth_in.at[n_gy * a + c],
            send_sem=w_send.at[2 * da + dc], recv_sem=w_recv.at[n_gy * a + c],
            device_id={"ta": to_a, "gy": to_c}, device_id_type=MESH_ID,
        )
        copy.start()
        w_copies.append(copy)
    smooth_in[n_gy * a + c] = smooth_out[c, a]
    for da, dc in ((0, 1), (1, 0), (1, 1)):
        slot = n_gy * lax.rem(a + da, n_ta) + lax.rem(c + dc, n_gy)
        pltpu.make_async_copy(smooth_in.at[slot], smooth_in.at[slot], w_recv.at[slot]).wait()

    def time_link(t):
        rows = []
        for r in range(2):
            tiles = [smooth_in[t, r, j] for j in range(3)]
            rows.append([(tile, pltpu.roll(tile, width - quarter, 1)) for tile in tiles])
        rows.append(third_row(rows[0], rows[1]))
        return rows

    early = times(time_link(0), time_link(1))
    late = times(time_link(2), time_link(3))
    re_terms, im_terms = [], []
    for i in range(3):
        for j in range(3):
            p_re, p_im = early[i][j]
            q_re, q_im = late[j][i]
            re_terms += [(1, p_re * q_re), (-1, p_im * q_im)]
            im_terms += [(1, p_re * q_im), (1, p_im * q_re)]
    trace_re = signed_sum(re_terms) / 3.0
    trace_im = signed_sum(im_terms) / 3.0
    trace_out[0] = trace_re
    trace_out[1] = trace_im
    sum_re = jnp.sum(jnp.where(inside, trace_re, 0.0), axis=0, keepdims=True)
    sum_im = jnp.sum(jnp.where(inside, trace_im, 0.0), axis=0, keepdims=True)
    both_re = sum_re + pltpu.roll(sum_re, seg, 1)
    both_im = sum_im + pltpu.roll(sum_im, seg, 1)
    sums = jnp.where(lane[0:1] < seg, both_re, both_im)
    row_out[0] = sums

    targets = []
    for s in range(2):
        for ta in range(n_ta):
            z = 2 * s + c
            is_self = (z == k) & (a == ta) & (a == c)
            remote = pltpu.make_async_remote_copy(
                src_ref=trace_out, dst_ref=traces.at[k],
                send_sem=t_send.at[s, ta], recv_sem=t_recv.at[k],
                device_id={"ta": ta, "gz": z, "gy": a}, device_id_type=MESH_ID,
            )
            local = pltpu.make_async_copy(trace_out, traces.at[k], t_recv.at[k])
            targets.append((is_self, remote))
            pl.when(jnp.logical_not(is_self))(remote.start)
            pl.when(is_self)(local.start)
    row_copies = []
    for step in range(1, n_group):
        copy = pltpu.make_async_remote_copy(
            src_ref=row_out, dst_ref=rows_in.at[pl.ds(step, 1)],
            send_sem=r_send.at[step], recv_sem=r_recv.at[step],
            device_id=peer(step), device_id_type=MESH_ID,
        )
        copy.start()
        row_copies.append(copy)

    for z in range(n_gz):
        pltpu.make_async_copy(traces.at[z], traces.at[z], t_recv.at[z]).wait()
    s_me = k // 2
    for ri in range(2):
        out = None
        for z in range(n_gz):
            shift = lax.rem(quarter * z + 2 * width - seg * s_me - HALO, width)
            piece = pltpu.roll(traces[z, ri], shift, 1)
            out = piece if out is None else jnp.where(lane >= quarter * z, piece, out)
        poly_ref[ri] = out
    total = sums
    for copy in row_copies:
        copy.wait_recv()
    for step in range(1, n_group):
        total = total + rows_in[step]
    mean_ref[0] = jnp.sum(jnp.where(lane[0:1] < seg, total, 0.0)) / sites
    mean_ref[1] = jnp.sum(jnp.where(lane[0:1] >= seg, total, 0.0)) / sites

    for group in range(len(groups)):
        for hop in hops:
            for t_rel in range(2):
                if hop or t_rel:
                    exchange(hop, t_rel, group).wait_send()
    for copy in next_copies:
        copy.wait_send()
    for copy in w_copies:
        copy.wait_send()
    for is_self, remote in targets:
        pl.when(jnp.logical_not(is_self))(remote.wait_send)
    for copy in row_copies:
        copy.wait_send()


def fused_on_device(mesh_shape, spatial_links, time_links):
    n_ta, n_gz, n_gy = (mesh_shape[name] for name in ("ta", "gz", "gy"))
    width = spatial_links.shape[-1]
    n_group = n_ta * n_gz * n_gy
    sites = float(n_gz * n_gy * 8 * width)
    spatial = spatial_links.reshape(3, 2, 3, 3, 2, 8, width)
    times_in = time_links.reshape(2, 3, 3, 2, 8, width)
    vm = lambda *shape: pltpu.VMEM(shape + (8, width), jnp.float32)
    dma = pltpu.SemaphoreType.DMA
    poly, mean = pl.pallas_call(
        partial(fused_kernel, (n_ta, n_gz, n_gy, width, sites)),
        out_shape=(
            jax.ShapeDtypeStruct((2, 8, width), jnp.float32),
            jax.ShapeDtypeStruct((2,), jnp.float32),
        ),
        in_specs=[pl.BlockSpec(memory_space=pl.ANY)] * 2,
        out_specs=(
            pl.BlockSpec(memory_space=pltpu.VMEM),
            pl.BlockSpec(memory_space=pltpu.SMEM),
        ),
        scratch_shapes=[
            vm(4, 2, 3, 3, 2),
            vm(n_gz, 2, 4, 2, 2),
            vm(n_gz, 2, 4, 2, 2),
            vm(4, 2, 3, 3, 2, 2),
            vm(6, 2, 2, 3, 2, 2),
            vm(6, 2, 2, 3, 2, 2),
            vm(3, n_gz, 2, 2, 2),
            vm(3, n_gz, 2, 2, 2),
            vm(2, 2, 2, 3),
            vm(4, 2, 3),
            vm(2),
            vm(n_gz, 2),
            pltpu.VMEM((1, 1, width), jnp.float32),
            pltpu.VMEM((n_group, 1, width), jnp.float32),
            dma((4,)),
            dma((3, n_gz, 2)), dma((3, n_gz, 2)),
            dma((3,)), dma((3,)), dma((4,)), dma((4,)),
            dma((2, n_ta)), dma((n_gz,)),
            dma((n_group,)), dma((n_group,)),
        ],
        compiler_params=pltpu.CompilerParams(collective_id=0, has_side_effects=True),
    )(spatial, times_in)
    return poly.reshape(2, 1, 8, width), mean


def fits_fused(mesh_shape, shape):
    width = shape[-1]
    n_ta, n_gz, n_gy = (mesh_shape[name] for name in ("ta", "gz", "gy"))
    per = shape[4] // n_ta, shape[5] // n_gz, shape[6] // n_gy
    window = width // n_gz + 2 * HALO
    return (
        per == (2, 1, 8) and n_ta == 2 and n_gz == 4 and n_gy == 2
        and width == 128 and ITERS >= 2 and 3 * window <= width and 2 * window <= width
    )


def solution(mesh):
    placed = (
        P("cfg", None, None, None, "ta", "gz", "gy", None),
        P("cfg", None, None, "ta", "gz", "gy", None),
    )

    def run(spatial_links, time_links):
        fused = fits_fused(mesh.shape, spatial_links.shape)
        body = partial(fused_on_device, dict(mesh.shape)) if fused else on_device
        return jax.shard_map(
            body,
            mesh=mesh,
            in_specs=placed,
            out_specs=(P("cfg", "gz", "gy", None), P("cfg")),
            check_vma=False,
        )(spatial_links, time_links)

    return run
```

profile of v0, /device:TPU:0, one launch (start us, length us, event | category | flops | bytes accessed | tf_op | source)
XLA Modules:
  0.0 42.8 jit_solution(9394437414331397507)
XLA Ops:
  0.6 40.3 %shard_map.41 = (f32[2,8,128]{2,1,0:T(8,128)}, f32[2]{0:T(128)}) custom-call(f32[3,2,3,3,2,8,128]{6,5,4,3,2,1,0:T(8,128)} %bitcast.5, f32[2,3,3,2,8,128]{5,4,3,2,1,0:T(8,128)} %bitcast.6), custom_call_target="tpu_custom_call" | custom-call | tf_op jit(solution)/shard_map/pallas_call | solution.py:662
  40.9 0.0 copy-start
  40.9 1.3 %copy.7 = f32[2,1,8,128]{3,2,1,0:T(8,128)} copy(f32[2,1,8,128]{3,2,1,0:T(8,128)} %bitcast.7) | data formatting | bytes 16384
  42.2 0.0 copy-done
  42.2 0.5 %copy.8 = f32[2]{0:T(128)} copy(f32[2]{0:T(128)S(1)} %copy-done) | data formatting | bytes 16
Async XLA Ops:
  40.9 1.3 %copy-start = (f32[2]{0:T(128)S(1)}, f32[2]{0:T(128)}, u32[]{:S(2)}) copy-start(f32[2]{0:T(128)} %get-tuple-element.11) | copy-start | bytes 28
where the time goes:
time: 42.9 us; the launch traced here: 42.8 us
  Pallas kernels  40.3 us (94%)
  local copies, waits for them, and re-layouts  1.81 us (4%)
  between operations  0.65 us (2%)
    pallas_call x1, Pallas kernels, fused_on_device(): pl.pallas_call(partial(fused_kernel, (n_ta, n_gz, n_gy, width, sites)), o...  40.3 us
    unnamed x4, local copies, waits for them, and re-layouts  1.81 us

commit v1 on v0

--- a/solution.py
+++ b/solution.py
@@ -275,7 +275,7 @@
     raw, packed, landed, state, ups, lows, outgoing, ahead, smooth_out, smooth_in,
     trace_out, traces, row_out, rows_in,
     load_sem, a_send, a_recv, n_send, n_recv, w_send, w_recv,
-    t_send, t_recv, r_send, r_recv,
+    t_send, t_recv, r_send, r_recv, near_sem, far_sem, side_sem,
 ):
     n_ta, n_gz, n_gy, width, sites = dims
     quarter = width // n_gz
@@ -285,25 +285,34 @@
     lane = lax.broadcasted_iota(jnp.int32, (8, width), 1)
     row_id = lax.broadcasted_iota(jnp.int32, (8, width), 0)
     n_group = n_ta * n_gz * n_gy
-    my_rank = (a * n_gz + k) * n_gy + c
+    middle = lax.rem((k + 1) // 2, 2)
+    far_half = k // 2
+
+    def mirrored(z):
+        return z + far_half * (n_gz - 1 - 2 * z)
+
+    barrier = pltpu.get_barrier_semaphore()
+
+    def greet(device):
+        pl.semaphore_signal(barrier, inc=1, device_id=device, device_id_type=MESH_ID)
+
+    def tell(sem, z):
+        pl.semaphore_signal(sem, inc=1, device_id={"gz": z}, device_id_type=MESH_ID)
+
+    greet({"gy": 1 - c})
+    greet({"ta": 1 - a})
+    for core in range(n_gy):
+        greet({"gz": mirrored(middle + 1), "gy": core})
+
+    @pl.when(middle == 1)
+    def _():
+        for core in range(n_gy):
+            greet({"gz": mirrored(0), "gy": core})
 
     loads = [pltpu.make_async_copy(sl_hbm.at[d], raw.at[d], load_sem.at[d]) for d in range(3)]
     loads.append(pltpu.make_async_copy(tl_hbm, raw.at[3], load_sem.at[3]))
     for copy in loads:
         copy.start()
-
-    def peer(step):
-        rank = lax.rem(my_rank + step, n_group)
-        return {
-            "ta": rank // (n_gz * n_gy),
-            "gz": lax.rem(rank // n_gy, n_gz),
-            "gy": lax.rem(rank, n_gy),
-        }
-
-    barrier = pltpu.get_barrier_semaphore()
-    for step in range(1, n_group):
-        pl.semaphore_signal(barrier, inc=1, device_id=peer(step), device_id_type=MESH_ID)
-
     wide = lax.broadcasted_iota(jnp.int32, (32, width), 1)
 
     def side_by_side(blocks, shift_of):
@@ -313,8 +322,11 @@
             tile = moved_block if j == 0 else jnp.where(wide >= window * j, moved_block, tile)
         return tile.reshape(2, 2, 8, width)
 
+    dests = [mirrored(middle + 1), mirrored(2 - 2 * middle), mirrored(3), k]
+    own = len(dests) - 1
+
     def pack(hop, d):
-        dest = lax.rem(k + hop, n_gz)
+        dest = dests[hop]
         for t in range(2):
             blocks = [raw[d, :, 0:2, j, t] for j in range(3)]
             packed[hop, t, d] = side_by_side(
@@ -325,33 +337,51 @@
     groups = ((0, 1), (2,), (3,))
 
     def exchange(hop, t_rel, group):
-        dest = lax.rem(k + hop, n_gz)
         t = lax.rem(c + t_rel, 2)
         part = pl.ds(groups[group][0], len(groups[group]))
         src = packed.at[hop, t, part]
         dst = landed.at[k, c, part]
-        if hop == 0 and t_rel == 0:
+        if hop == own and t_rel == 0:
             return pltpu.make_async_copy(src, dst, a_recv.at[group, k, c])
         return pltpu.make_async_remote_copy(
             src_ref=src, dst_ref=dst,
             send_sem=a_send.at[group, hop, t_rel], recv_sem=a_recv.at[group, k, c],
-            device_id={"gz": dest, "gy": t}, device_id_type=MESH_ID,
+            device_id={"gz": dests[hop], "gy": t}, device_id_type=MESH_ID,
         )
 
-    hops = [2, 3, 1, 0]
-    waited = False
+    hops = list(range(len(dests)))
     for group, members in enumerate(groups):
         for d in members:
             loads[d].wait()
         for d in members:
-            pack(hops[0], d)
-        if not waited:
-            pl.semaphore_wait(barrier, n_group - 1)
-            waited = True
-        for n, hop in enumerate(hops):
-            if n + 1 < len(hops):
+            pack(0, d)
+        if group == 0:
+            pl.semaphore_wait(barrier, 4 + 2 * middle)
+
+            @pl.when(middle == 1)
+            def _():
+                tell(near_sem, mirrored(0))
+                tell(far_sem, mirrored(2))
+        for hop in hops:
+            if hop:
                 for d in members:
-                    pack(hops[n + 1], d)
+                    pack(hop, d)
+            if group == 0 and hop == 1:
+
+                @pl.when(middle == 0)
+                def _():
+                    pl.semaphore_wait(near_sem, 1)
+
+            if group == 0 and hop == 2:
+                pl.semaphore_wait(far_sem, 1)
+
+                @pl.when(middle == 1)
+                def _():
+                    tell(far_sem, mirrored(0))
+
+                pl.semaphore_signal(
+                    side_sem, inc=1, device_id={"ta": 1 - a}, device_id_type=MESH_ID
+                )
             for t_rel in range(2):
                 exchange(hop, t_rel, group).start()
 
@@ -473,7 +503,6 @@
         staples(pairs)
         update((0, 1, 2))
         return carry
-
     arrived(0)
     unpack(0)
     unpack(1)
@@ -503,7 +532,7 @@
                         blocks, lambda j: (window * j + width - seg * s) % width
                     )
         next_copies[mu].start()
-
+    pl.semaphore_wait(side_sem, 1)
     staples(pairs[0:2])
     update((0,))
     send_next(0)
@@ -535,32 +564,28 @@
     place = lax.rem(lane, seg)
     inside = (place >= HALO) & (place < HALO + quarter)
 
-    def smooth_at(index, carry):
-        v, h = index // 2, lax.rem(index, 2)
+    def smooth(v, h, out_ref):
         mat = mix(3, v, h, [(nu, nu) for nu in range(3)], smear_weight / 6.0)
         for r in range(2):
             for j in range(3):
                 re, im = mat[r][j]
-                smooth_out[v, h, r, j] = jnp.where(inside, re, pltpu.roll(im, quarter, 1))
-        return carry
-
+                out_ref[r, j] = jnp.where(inside, re, pltpu.roll(im, quarter, 1))
     lax.fori_loop(0, 4, time_firsts_at, 0)
     for nu in range(3):
         next_copies[nu].wait_recv()
         lax.fori_loop(0, 4, partial(time_staples_at, nu), 0)
-    lax.fori_loop(0, 4, smooth_at, 0)
-
     w_copies = []
     for da, dc in ((1, 0), (1, 1), (0, 1)):
         to_a, to_c = lax.rem(a + da, n_ta), lax.rem(c + dc, n_gy)
+        smooth(to_c, to_a, smooth_out.at[2 * da + dc])
         copy = pltpu.make_async_remote_copy(
-            src_ref=smooth_out.at[to_c, to_a], dst_ref=smooth_in.at[n_gy * a + c],
+            src_ref=smooth_out.at[2 * da + dc], dst_ref=smooth_in.at[n_gy * a + c],
             send_sem=w_send.at[2 * da + dc], recv_sem=w_recv.at[n_gy * a + c],
             device_id={"ta": to_a, "gy": to_c}, device_id_type=MESH_ID,
         )
         copy.start()
         w_copies.append(copy)
-    smooth_in[n_gy * a + c] = smooth_out[c, a]
+    smooth(c, a, smooth_in.at[n_gy * a + c])
     for da, dc in ((0, 1), (1, 0), (1, 1)):
         slot = n_gy * lax.rem(a + da, n_ta) + lax.rem(c + dc, n_gy)
         pltpu.make_async_copy(smooth_in.at[slot], smooth_in.at[slot], w_recv.at[slot]).wait()
@@ -572,7 +597,6 @@
             rows.append([(tile, pltpu.roll(tile, width - quarter, 1)) for tile in tiles])
         rows.append(third_row(rows[0], rows[1]))
         return rows
-
     early = times(time_link(0), time_link(1))
     late = times(time_link(2), time_link(3))
     re_terms, im_terms = [], []
@@ -592,7 +616,6 @@
     both_im = sum_im + pltpu.roll(sum_im, seg, 1)
     sums = jnp.where(lane[0:1] < seg, both_re, both_im)
     row_out[0] = sums
-
     targets = []
     for s in range(2):
         for ta in range(n_ta):
@@ -609,10 +632,16 @@
             pl.when(is_self)(local.start)
     row_copies = []
     for step in range(1, n_group):
+        da, dk, dc = step // (n_gz * n_gy), step // n_gy % n_gz, step % n_gy
+        device = {
+            "ta": lax.rem(a + da, n_ta),
+            "gz": lax.rem(k + dk, n_gz),
+            "gy": lax.rem(c + dc, n_gy),
+        }
         copy = pltpu.make_async_remote_copy(
             src_ref=row_out, dst_ref=rows_in.at[pl.ds(step, 1)],
             send_sem=r_send.at[step], recv_sem=r_recv.at[step],
-            device_id=peer(step), device_id_type=MESH_ID,
+            device_id=device, device_id_type=MESH_ID,
         )
         copy.start()
         row_copies.append(copy)
@@ -634,11 +663,10 @@
         total = total + rows_in[step]
     mean_ref[0] = jnp.sum(jnp.where(lane[0:1] < seg, total, 0.0)) / sites
     mean_ref[1] = jnp.sum(jnp.where(lane[0:1] >= seg, total, 0.0)) / sites
-
     for group in range(len(groups)):
         for hop in hops:
             for t_rel in range(2):
-                if hop or t_rel:
+                if hop != own or t_rel:
                     exchange(hop, t_rel, group).wait_send()
     for copy in next_copies:
         copy.wait_send()
@@ -648,6 +676,10 @@
         pl.when(jnp.logical_not(is_self))(remote.wait_send)
     for copy in row_copies:
         copy.wait_send()
+def hand_over(poly_in, mean_in, poly_ref, mean_ref):
+    poly_ref[...] = poly_in[...]
+    for ri in range(2):
+        mean_ref[ri] = mean_in[ri]
 
 
 def fused_on_device(mesh_shape, spatial_links, time_links):
@@ -679,7 +711,7 @@
             vm(6, 2, 2, 3, 2, 2),
             vm(3, n_gz, 2, 2, 2),
             vm(3, n_gz, 2, 2, 2),
-            vm(2, 2, 2, 3),
+            vm(4, 2, 3),
             vm(4, 2, 3),
             vm(2),
             vm(n_gz, 2),
@@ -690,9 +722,25 @@
             dma((3,)), dma((3,)), dma((4,)), dma((4,)),
             dma((2, n_ta)), dma((n_gz,)),
             dma((n_group,)), dma((n_group,)),
+            *[pltpu.SemaphoreType.REGULAR] * 3,
         ],
         compiler_params=pltpu.CompilerParams(collective_id=0, has_side_effects=True),
     )(spatial, times_in)
+    poly, mean = pl.pallas_call(
+        hand_over,
+        out_shape=(
+            jax.ShapeDtypeStruct((2, 8, width), jnp.float32),
+            jax.ShapeDtypeStruct((2,), jnp.float32),
+        ),
+        in_specs=[
+            pl.BlockSpec(memory_space=pltpu.VMEM),
+            pl.BlockSpec(memory_space=pltpu.SMEM),
+        ],
+        out_specs=(
+            pl.BlockSpec(memory_space=pltpu.VMEM),
+            pl.BlockSpec(memory_space=pltpu.SMEM),
+        ),
+    )(poly, mean)
     return poly.reshape(2, 1, 8, width), mean
 
 

time: 42.9 us -> 41 us (0.956)
  local copies, waits for them, and re-layouts: 1.81 us -> 0 us
    unnamed x4 -> x0, local copies, waits for them, and re-layouts: 1.81 us -> none
    pallas_call x1, Pallas kernels: 40.3 us -> 38.7 us  [fused_on_device(): pl.pallas_call(partial(fused_kernel, (n_ta, n_gz, n_gy, width, sites)), o...]
    pallas_call x0 -> x1, Pallas kernels: none -> 1.41 us  [fused_on_device(): pl.pallas_call(hand_over, out_shape=(jax.ShapeDtypeStruct((2, 8, width),...]
where the time goes in v1:
time: 41 us; the launch traced here: 40.8 us
  Pallas kernels  40.1 us (98%)
  between operations  0.64 us (2%)
    pallas_call x1, Pallas kernels, fused_on_device(): pl.pallas_call(partial(fused_kernel, (n_ta, n_gz, n_gy, width, sites)), o...  38.7 us
    pallas_call x1, Pallas kernels, fused_on_device(): pl.pallas_call(hand_over, out_shape=(jax.ShapeDtypeStruct((2, 8, width),...  1.41 us

profile of v1, /device:TPU:0, one launch (start us, length us, event | category | flops | bytes accessed | tf_op | source)
XLA Modules:
  0.0 40.8 jit_solution(13496900547436067877)
XLA Ops:
  0.6 38.7 %shard_map.41 = (f32[2,8,128]{2,1,0:T(8,128)}, f32[2]{0:T(128)}) custom-call(f32[3,2,3,3,2,8,128]{6,5,4,3,2,1,0:T(8,128)} %bitcast.5, f32[2,3,3,2,8,128]{5,4,3,2,1,0:T(8,128)} %bitcast.6), custom_call_target="tpu_custom_call" | custom-call | tf_op jit(solution)/shard_map/pallas_call | solution.py:694
  39.4 1.4 %shard_map.42 = (f32[2,8,128]{2,1,0:T(8,128)}, f32[2]{0:T(128)}) custom-call(f32[2,8,128]{2,1,0:T(8,128)} %get-tuple-element.6.poly_in, f32[2]{0:T(128)} %get-tuple-element.7.mean_in), custom_call_target="tpu_custom_call" | custom-call | tf_op jit(solution)/shard_map/pallas_call | solution.py:729

commit v2 on v1

--- a/solution.py
+++ b/solution.py
@@ -271,7 +271,7 @@
 
 
 def fused_kernel(
-    dims, sl_hbm, tl_hbm, poly_ref, mean_ref,
+    dims, sl_hbm, tl_hbm, poly_ref, total_ref,
     raw, packed, landed, state, ups, lows, outgoing, ahead, smooth_out, smooth_in,
     trace_out, traces, row_out, rows_in,
     load_sem, a_send, a_recv, n_send, n_recv, w_send, w_recv,
@@ -313,6 +313,9 @@
     loads.append(pltpu.make_async_copy(tl_hbm, raw.at[3], load_sem.at[3]))
     for copy in loads:
         copy.start()
+    def settle(ref, sem):
+        pltpu.make_async_copy(ref, ref, sem).wait()
+
     wide = lax.broadcasted_iota(jnp.int32, (32, width), 1)
 
     def side_by_side(blocks, shift_of):
@@ -342,15 +345,17 @@
         src = packed.at[hop, t, part]
         dst = landed.at[k, c, part]
         if hop == own and t_rel == 0:
-            return pltpu.make_async_copy(src, dst, a_recv.at[group, k, c])
+            return pltpu.make_async_copy(src, dst, a_recv.at[group])
         return pltpu.make_async_remote_copy(
             src_ref=src, dst_ref=dst,
-            send_sem=a_send.at[group, hop, t_rel], recv_sem=a_recv.at[group, k, c],
+            send_sem=a_send.at[hop // own], recv_sem=a_recv.at[group],
             device_id={"gz": dests[hop], "gy": t}, device_id_type=MESH_ID,
         )
 
     hops = list(range(len(dests)))
-    for group, members in enumerate(groups):
+
+    def hand_out(group):
+        members = groups[group]
         for d in members:
             loads[d].wait()
         for d in members:
@@ -385,12 +390,12 @@
             for t_rel in range(2):
                 exchange(hop, t_rel, group).start()
 
+    hand_out(0)
+    hand_out(1)
+
     def arrived(group):
         part = pl.ds(groups[group][0], len(groups[group]))
-        for z in range(n_gz):
-            for h in range(2):
-                ref = landed.at[z, h, part]
-                pltpu.make_async_copy(ref, ref, a_recv.at[group, z, h]).wait()
+        settle(landed.at[:, :, part], a_recv.at[group])
 
     def spread(read, v, h):
         rows = []
@@ -508,6 +513,7 @@
     unpack(1)
     staples(pairs[0:1])
     arrived(1)
+    hand_out(2)
     unpack(2)
     staples(pairs[1:3])
     update((0, 1, 2))
@@ -516,7 +522,7 @@
     next_copies = [
         pltpu.make_async_remote_copy(
             src_ref=outgoing.at[mu], dst_ref=ahead.at[mu],
-            send_sem=n_send.at[mu], recv_sem=n_recv.at[mu],
+            send_sem=n_send.at[0], recv_sem=n_recv.at[mu],
             device_id={"ta": lax.rem(a + c + n_ta - 1, n_ta), "gy": 1 - c},
             device_id_type=MESH_ID,
         )
@@ -574,21 +580,17 @@
     for nu in range(3):
         next_copies[nu].wait_recv()
         lax.fori_loop(0, 4, partial(time_staples_at, nu), 0)
-    w_copies = []
     for da, dc in ((1, 0), (1, 1), (0, 1)):
         to_a, to_c = lax.rem(a + da, n_ta), lax.rem(c + dc, n_gy)
         smooth(to_c, to_a, smooth_out.at[2 * da + dc])
         copy = pltpu.make_async_remote_copy(
             src_ref=smooth_out.at[2 * da + dc], dst_ref=smooth_in.at[n_gy * a + c],
-            send_sem=w_send.at[2 * da + dc], recv_sem=w_recv.at[n_gy * a + c],
+            send_sem=w_send.at[0], recv_sem=w_recv.at[0],
             device_id={"ta": to_a, "gy": to_c}, device_id_type=MESH_ID,
         )
         copy.start()
-        w_copies.append(copy)
     smooth(c, a, smooth_in.at[n_gy * a + c])
-    for da, dc in ((0, 1), (1, 0), (1, 1)):
-        slot = n_gy * lax.rem(a + da, n_ta) + lax.rem(c + dc, n_gy)
-        pltpu.make_async_copy(smooth_in.at[slot], smooth_in.at[slot], w_recv.at[slot]).wait()
+    settle(smooth_out.at[pl.ds(1, n_ta * n_gy - 1)], w_recv.at[0])
 
     def time_link(t):
         rows = []
@@ -616,21 +618,19 @@
     both_im = sum_im + pltpu.roll(sum_im, seg, 1)
     sums = jnp.where(lane[0:1] < seg, both_re, both_im)
     row_out[0] = sums
-    targets = []
+    keeps_one = (a == c) & (lax.rem(k, 2) == c)
     for s in range(2):
         for ta in range(n_ta):
             z = 2 * s + c
             is_self = (z == k) & (a == ta) & (a == c)
             remote = pltpu.make_async_remote_copy(
                 src_ref=trace_out, dst_ref=traces.at[k],
-                send_sem=t_send.at[s, ta], recv_sem=t_recv.at[k],
+                send_sem=t_send.at[0], recv_sem=t_recv.at[0],
                 device_id={"ta": ta, "gz": z, "gy": a}, device_id_type=MESH_ID,
             )
-            local = pltpu.make_async_copy(trace_out, traces.at[k], t_recv.at[k])
-            targets.append((is_self, remote))
+            local = pltpu.make_async_copy(trace_out, traces.at[k], t_recv.at[0])
             pl.when(jnp.logical_not(is_self))(remote.start)
             pl.when(is_self)(local.start)
-    row_copies = []
     for step in range(1, n_group):
         da, dk, dc = step // (n_gz * n_gy), step // n_gy % n_gz, step % n_gy
         device = {
@@ -640,14 +640,12 @@
         }
         copy = pltpu.make_async_remote_copy(
             src_ref=row_out, dst_ref=rows_in.at[pl.ds(step, 1)],
-            send_sem=r_send.at[step], recv_sem=r_recv.at[step],
+            send_sem=r_send.at[0], recv_sem=r_recv.at[0],
             device_id=device, device_id_type=MESH_ID,
         )
         copy.start()
-        row_copies.append(copy)
-
-    for z in range(n_gz):
-        pltpu.make_async_copy(traces.at[z], traces.at[z], t_recv.at[z]).wait()
+
+    settle(traces, t_recv.at[0])
     s_me = k // 2
     for ri in range(2):
         out = None
@@ -657,29 +655,31 @@
             out = piece if out is None else jnp.where(lane >= quarter * z, piece, out)
         poly_ref[ri] = out
     total = sums
-    for copy in row_copies:
-        copy.wait_recv()
+    settle(rows_in.at[pl.ds(1, n_group - 1)], r_recv.at[0])
     for step in range(1, n_group):
         total = total + rows_in[step]
-    mean_ref[0] = jnp.sum(jnp.where(lane[0:1] < seg, total, 0.0)) / sites
-    mean_ref[1] = jnp.sum(jnp.where(lane[0:1] >= seg, total, 0.0)) / sites
-    for group in range(len(groups)):
-        for hop in hops:
-            for t_rel in range(2):
-                if hop != own or t_rel:
-                    exchange(hop, t_rel, group).wait_send()
-    for copy in next_copies:
-        copy.wait_send()
-    for copy in w_copies:
-        copy.wait_send()
-    for is_self, remote in targets:
-        pl.when(jnp.logical_not(is_self))(remote.wait_send)
-    for copy in row_copies:
-        copy.wait_send()
-def hand_over(poly_in, mean_in, poly_ref, mean_ref):
+    total_ref[...] = total
+    settle(packed.at[pl.ds(0, own)], a_send.at[0])
+    settle(packed.at[own, 0], a_send.at[1])
+    settle(outgoing, n_send.at[0])
+    settle(smooth_out.at[pl.ds(1, n_ta * n_gy - 1)], w_send.at[0])
+
+    @pl.when(keeps_one)
+    def _():
+        settle(traces.at[pl.ds(1, n_gz - 1)], t_send.at[0])
+
+    @pl.when(jnp.logical_not(keeps_one))
+    def _():
+        settle(traces, t_send.at[0])
+
+    settle(rows_in.at[pl.ds(1, n_group - 1)], r_send.at[0])
+def hand_over(sites, poly_in, total_in, poly_ref, mean_ref):
     poly_ref[...] = poly_in[...]
-    for ri in range(2):
-        mean_ref[ri] = mean_in[ri]
+    total = total_in[...]
+    seg = total.shape[1] // 2
+    place = lax.broadcasted_iota(jnp.int32, total.shape, 1)
+    mean_ref[0] = jnp.sum(jnp.where(place < seg, total, 0.0)) / sites
+    mean_ref[1] = jnp.sum(jnp.where(place >= seg, total, 0.0)) / sites
 
 
 def fused_on_device(mesh_shape, spatial_links, time_links):
@@ -691,17 +691,14 @@
     times_in = time_links.reshape(2, 3, 3, 2, 8, width)
     vm = lambda *shape: pltpu.VMEM(shape + (8, width), jnp.float32)
     dma = pltpu.SemaphoreType.DMA
-    poly, mean = pl.pallas_call(
+    poly, total = pl.pallas_call(
         partial(fused_kernel, (n_ta, n_gz, n_gy, width, sites)),
         out_shape=(
-            jax.ShapeDtypeStruct((2, 8, width), jnp.float32),
-            jax.ShapeDtypeStruct((2,), jnp.float32),
+            pltpu.VMEM((2, 8, width), jnp.float32),
+            pltpu.VMEM((1, width), jnp.float32),
         ),
         in_specs=[pl.BlockSpec(memory_space=pl.ANY)] * 2,
-        out_specs=(
-            pl.BlockSpec(memory_space=pltpu.VMEM),
-            pl.BlockSpec(memory_space=pltpu.SMEM),
-        ),
+        out_specs=(pl.BlockSpec(memory_space=pltpu.VMEM),) * 2,
         scratch_shapes=[
             vm(4, 2, 3, 3, 2),
             vm(n_gz, 2, 4, 2, 2),
@@ -718,29 +715,24 @@
             pltpu.VMEM((1, 1, width), jnp.float32),
             pltpu.VMEM((n_group, 1, width), jnp.float32),
             dma((4,)),
-            dma((3, n_gz, 2)), dma((3, n_gz, 2)),
-            dma((3,)), dma((3,)), dma((4,)), dma((4,)),
-            dma((2, n_ta)), dma((n_gz,)),
-            dma((n_group,)), dma((n_group,)),
+            dma((2,)), dma((3,)), dma((1,)), dma((3,)),
+            *[dma((1,))] * 6,
             *[pltpu.SemaphoreType.REGULAR] * 3,
         ],
         compiler_params=pltpu.CompilerParams(collective_id=0, has_side_effects=True),
     )(spatial, times_in)
     poly, mean = pl.pallas_call(
-        hand_over,
+        partial(hand_over, sites),
         out_shape=(
             jax.ShapeDtypeStruct((2, 8, width), jnp.float32),
             jax.ShapeDtypeStruct((2,), jnp.float32),
         ),
-        in_specs=[
-            pl.BlockSpec(memory_space=pltpu.VMEM),
-            pl.BlockSpec(memory_space=pltpu.SMEM),
-        ],
+        in_specs=[pl.BlockSpec(memory_space=pltpu.VMEM)] * 2,
         out_specs=(
             pl.BlockSpec(memory_space=pltpu.VMEM),
             pl.BlockSpec(memory_space=pltpu.SMEM),
         ),
-    )(poly, mean)
+    )(*[pltpu.with_memory_space_constraint(x, pltpu.VMEM) for x in (poly, total)])
     return poly.reshape(2, 1, 8, width), mean
 
 

time: 41 us -> 37.6 us (0.917)
  Pallas kernels: 40.1 us -> 36.8 us
    pallas_call x1, Pallas kernels: 38.7 us -> 36.1 us  [fused_on_device(): pl.pallas_call(partial(fused_kernel, (n_ta, n_gz, n_gy, width, sites)), o...]
    pallas_call x1, Pallas kernels: 1.41 us -> 0.64 us  [fused_on_device(): pl.pallas_call(partial(hand_over, sites), out_shape=(jax.ShapeDtypeStruct...]
where the time goes in v2:
time: 37.6 us; the launch traced here: 37.4 us
  Pallas kernels  36.8 us (98%)
  between operations  0.64 us (2%)
    pallas_call x1, Pallas kernels, fused_on_device(): pl.pallas_call(partial(fused_kernel, (n_ta, n_gz, n_gy, width, sites)), o...  36.1 us

profile of v2, /device:TPU:0, one launch (start us, length us, event | category | flops | bytes accessed | tf_op | source)
XLA Modules:
  0.0 37.4 jit_solution(17663698435172445020)
XLA Ops:
  0.6 36.1 %shard_map.41 = (f32[2,8,128]{2,1,0:T(8,128)S(1)}, f32[1,128]{1,0:T(1,128)S(1)}) custom-call(f32[3,2,3,3,2,8,128]{6,5,4,3,2,1,0:T(8,128)} %bitcast.5, f32[2,3,3,2,8,128]{5,4,3,2,1,0:T(8,128)} %bitcast.6), custom_call_target="tpu_custom_call" | custom-call | tf_op jit(solution)/shard_map/pallas_call | solution.py:694
  36.8 0.6 %shard_map.42 = (f32[2,8,128]{2,1,0:T(8,128)}, f32[2]{0:T(128)}) custom-call(f32[2,8,128]{2,1,0:T(8,128)S(1)} %get-tuple-element.6.poly_in, f32[1,128]{1,0:T(1,128)S(1)} %get-tuple-element.7.total_in), custom_call_target="tpu_custom_call" | custom-call | tf_op jit(solution)/shard_map/pallas_call | solution.py:724

commit v3 on v2

--- a/solution.py
+++ b/solution.py
@@ -272,18 +272,17 @@
 
 def fused_kernel(
     dims, sl_hbm, tl_hbm, poly_ref, total_ref,
-    raw, packed, landed, state, ups, lows, outgoing, ahead, smooth_out, smooth_in,
+    raw, packed, landed, state, ups, lows, outgoing, ahead, ahead_x, smooth_out, smooth_in,
     trace_out, traces, row_out, rows_in,
     load_sem, a_send, a_recv, n_send, n_recv, w_send, w_recv,
     t_send, t_recv, r_send, r_recv, near_sem, far_sem, side_sem,
 ):
     n_ta, n_gz, n_gy, width, sites = dims
     quarter = width // n_gz
-    window = quarter + 2 * HALO
-    seg = width // 2
+    slot = width // 3
+    tiles = range(3)
     a, k, c = lax.axis_index("ta"), lax.axis_index("gz"), lax.axis_index("gy")
     lane = lax.broadcasted_iota(jnp.int32, (8, width), 1)
-    row_id = lax.broadcasted_iota(jnp.int32, (8, width), 0)
     n_group = n_ta * n_gz * n_gy
     middle = lax.rem((k + 1) // 2, 2)
     far_half = k // 2
@@ -322,7 +321,7 @@
         tile = None
         for j in range(3):
             moved_block = pltpu.roll(blocks[j].reshape(32, width), shift_of(j), 1)
-            tile = moved_block if j == 0 else jnp.where(wide >= window * j, moved_block, tile)
+            tile = moved_block if j == 0 else jnp.where(wide >= slot * j, moved_block, tile)
         return tile.reshape(2, 2, 8, width)
 
     dests = [mirrored(middle + 1), mirrored(2 - 2 * middle), mirrored(3), k]
@@ -334,7 +333,7 @@
             blocks = [raw[d, :, 0:2, j, t] for j in range(3)]
             packed[hop, t, d] = side_by_side(
                 blocks,
-                lambda j: lax.rem(window * j + HALO + width - quarter * dest + width, width),
+                lambda j: lax.rem(slot * j + HALO + width - quarter * dest + width, width),
             )
 
     groups = ((0, 1), (2,), (3,))
@@ -343,7 +342,7 @@
         t = lax.rem(c + t_rel, 2)
         part = pl.ds(groups[group][0], len(groups[group]))
         src = packed.at[hop, t, part]
-        dst = landed.at[k, c, part]
+        dst = landed.at[k, part, :, :, pl.ds(pl.multiple_of(8 * c, 8), 8)]
         if hop == own and t_rel == 0:
             return pltpu.make_async_copy(src, dst, a_recv.at[group])
         return pltpu.make_async_remote_copy(
@@ -395,70 +394,91 @@
 
     def arrived(group):
         part = pl.ds(groups[group][0], len(groups[group]))
-        settle(landed.at[:, :, part], a_recv.at[group])
-
-    def spread(read, v, h):
-        rows = []
-        for r in range(2):
-            line = []
-            for j in range(3):
-                pair = []
-                for ri in range(2):
-                    low = pltpu.roll(read(v, h, ri, r), (width - window * j) % width, 1)
-                    high = pltpu.roll(
-                        read(2 + v, h, ri, r), (width + seg - window * j) % width, 1
-                    )
-                    pair.append(jnp.where(lane < seg, low, high))
-                line.append(tuple(pair))
-            rows.append(line)
+        settle(landed.at[:, part], a_recv.at[group])
+
+    def turn(value, lanes):
+        lanes = lanes % width
+        return pltpu.roll(value, lanes, 1) if lanes else value
+
+    def by_slot(values):
+        tile = values[-1]
+        for g in reversed(range(len(values) - 1)):
+            tile = jnp.where(lane < slot * (g + 1), values[g], tile)
+        return tile
+
+    places = [[(z, 0) for z in range(3)], [(z, 1) for z in range(3)], [(3, 0), (3, 1)]]
+
+    def closed(read):
+        rows = [[(read(0, r, j), read(1, r, j)) for j in range(3)] for r in range(2)]
         rows.append(third_row(rows[0], rows[1]))
         return rows
 
     def unpack(d):
-        for v in range(2):
-            for h in range(2):
-                put(d, v, h, spread(lambda z, hh, ri, r: landed[z, hh, d, ri, r], v, h))
-
-    def put(d, v, h, mat):
+        for tile in tiles:
+
+            def entry(ri, r, j):
+                return by_slot([
+                    turn(landed[z, d, ri, r, pl.ds(h, 8, stride=2)], slot * (g - j))
+                    for g, (z, h) in enumerate(places[tile])
+                ])
+
+            put(d, tile, closed(entry))
+
+    def put(d, tile, mat):
         for r in range(3):
             for j in range(3):
                 for ri in range(2):
-                    state[d, ri, r, j, v, h] = mat[r][j][ri]
+                    state[d, ri, r, j, tile] = mat[r][j][ri]
 
     def get(read, rows=3):
         return [[(read(0, r, j), read(1, r, j)) for j in range(3)] for r in range(rows)]
 
-    def shift_plus(read, nu, v, h):
+    def down(value):
+        return pltpu.roll(value, 7, 0)
+
+    def up_row(value):
+        return pltpu.roll(value, 1, 0)
+
+    def shift_plus(read, nu, tile):
         if nu == 0:
-            return pltpu.roll(read(v, h), width - 1, 1)
+            return turn(read(tile), -1)
         if nu == 1:
-            return jnp.where(
-                row_id == 7, pltpu.roll(read(v, 1 - h), 7, 0), pltpu.roll(read(v, h), 7, 0)
-            )
-        return pltpu.roll(read(1 - v, h), seg * v, 1)
-
-    def shift_minus(read, nu, v, h):
+            if tile == 0:
+                return read(1)
+            if tile == 1:
+                return down(read(0))
+            return by_slot([turn(read(2), -slot), down(turn(read(2), slot))])
+        if tile == 2:
+            return by_slot([read(0), turn(read(1), slot)])
+        inner = turn(read(tile), -slot)
+        return jnp.where(lane < 2 * slot, inner, turn(read(2), slot * (2 - tile)))
+
+    def shift_minus(read, nu, tile):
         if nu == 0:
-            return pltpu.roll(read(v, h), 1, 1)
+            return turn(read(tile), 1)
         if nu == 1:
-            return jnp.where(
-                row_id == 0, pltpu.roll(read(v, 1 - h), 1, 0), pltpu.roll(read(v, h), 1, 0)
-            )
-        return pltpu.roll(read(1 - v, h), seg * (1 - v), 1)
-
-    def here(d, v, h):
-        return get(lambda ri, r, j: state[d, ri, r, j, v, h])
-
-    def plus(d, nu, v, h):
+            if tile == 0:
+                return up_row(read(1))
+            if tile == 1:
+                return read(0)
+            return by_slot([up_row(turn(read(2), -slot)), turn(read(2), slot)])
+        if tile == 2:
+            return by_slot([turn(read(0), -2 * slot), turn(read(1), -slot)])
+        return by_slot([turn(read(2), -slot * tile), turn(read(tile), slot)])
+
+    def here(d, tile):
+        return get(lambda ri, r, j: state[d, ri, r, j, tile])
+
+    def plus(d, nu, tile):
         return get(
-            lambda ri, r, j: shift_plus(lambda vv, hh: state[d, ri, r, j, vv, hh], nu, v, h)
+            lambda ri, r, j: shift_plus(lambda other: state[d, ri, r, j, other], nu, tile)
         )
 
-    def keep(ref, slot, v, h, mat):
+    def keep(ref, entry, tile, mat):
         for r in range(2):
             for j in range(3):
                 for ri in range(2):
-                    ref[slot, ri, r, j, v, h] = mat[r][j][ri]
+                    ref[entry, ri, r, j, tile] = mat[r][j][ri]
 
     pairs = [(0, 1), (0, 2), (1, 2)]
     slot_of = {}
@@ -467,77 +487,93 @@
             if mu != nu:
                 slot_of[mu, nu] = len(slot_of)
 
-    def staples_at(chosen, index, carry):
-        v, h = index // 2, lax.rem(index, 2)
-        for mu, nu in chosen:
-            u_mu, u_nu = here(mu, v, h), here(nu, v, h)
-            nu_ahead, mu_ahead = plus(nu, mu, v, h), plus(mu, nu, v, h)
-            one = times(u_mu, nu_ahead)
-            keep(lows, slot_of[mu, nu], v, h, times(u_nu, one, lhs_dag=True, rows=2))
-            keep(ups, slot_of[nu, mu], v, h, times(one, mu_ahead, rhs_dag=True, rows=2))
-            two = times(u_nu, mu_ahead)
-            keep(lows, slot_of[nu, mu], v, h, times(u_mu, two, lhs_dag=True, rows=2))
-            keep(ups, slot_of[mu, nu], v, h, times(two, nu_ahead, rhs_dag=True, rows=2))
-        return carry
-
-    def mix(d, v, h, entries, factor):
+    def staples(chosen):
+        for tile in tiles:
+            for mu, nu in chosen:
+                u_mu, u_nu = here(mu, tile), here(nu, tile)
+                nu_ahead, mu_ahead = plus(nu, mu, tile), plus(mu, nu, tile)
+                one = times(u_mu, nu_ahead)
+                keep(lows, slot_of[mu, nu], tile, times(u_nu, one, lhs_dag=True, rows=2))
+                keep(ups, slot_of[nu, mu], tile, times(one, mu_ahead, rhs_dag=True, rows=2))
+                two = times(u_nu, mu_ahead)
+                keep(lows, slot_of[nu, mu], tile, times(u_mu, two, lhs_dag=True, rows=2))
+                keep(ups, slot_of[mu, nu], tile, times(two, nu_ahead, rhs_dag=True, rows=2))
+
+    def mix(d, tile, entries, factor):
         def entry(ri, r, j):
             total = None
-            for slot, nu in entries:
-                low = shift_minus(lambda vv, hh: lows[slot, ri, r, j, vv, hh], nu, v, h)
-                part = ups[slot, ri, r, j, v, h] + low
+            for at, nu in entries:
+                low = shift_minus(lambda other: lows[at, ri, r, j, other], nu, tile)
+                part = ups[at, ri, r, j, tile] + low
                 total = part if total is None else total + part
-            return (1.0 - smear_weight) * state[d, ri, r, j, v, h] + factor * total
+            return (1.0 - smear_weight) * state[d, ri, r, j, tile] + factor * total
 
         return project_rows(get(entry, rows=2))
 
-    def update_at(chosen, index, carry):
-        v, h = index // 2, lax.rem(index, 2)
-        for mu in chosen:
-            entries = [(slot_of[mu, nu], nu) for nu in range(3) if nu != mu]
-            put(mu, v, h, mix(mu, v, h, entries, smear_weight / 4.0))
-        return carry
-
-    def staples(chosen):
-        lax.fori_loop(0, 4, partial(staples_at, chosen), 0)
-
     def update(chosen):
-        lax.fori_loop(0, 4, partial(update_at, chosen), 0)
-
-    def sweep(index, carry):
-        staples(pairs)
-        update((0, 1, 2))
-        return carry
+        for tile in tiles:
+            for mu in chosen:
+                entries = [(slot_of[mu, nu], nu) for nu in range(3) if nu != mu]
+                put(mu, tile, mix(mu, tile, entries, smear_weight / 4.0))
     arrived(0)
     unpack(0)
     unpack(1)
-    staples(pairs[0:1])
-    arrived(1)
-    hand_out(2)
-    unpack(2)
-    staples(pairs[1:3])
-    update((0, 1, 2))
-    lax.fori_loop(0, ITERS - 2, sweep, 0)
-
-    next_copies = [
-        pltpu.make_async_remote_copy(
-            src_ref=outgoing.at[mu], dst_ref=ahead.at[mu],
-            send_sem=n_send.at[0], recv_sem=n_recv.at[mu],
+
+    def sweep(index, carry):
+        staples(pairs[0:1])
+
+        @pl.when(index == 0)
+        def _():
+            arrived(1)
+            hand_out(2)
+            unpack(2)
+
+        staples(pairs[1:3])
+        update((0, 1, 2))
+        return carry
+    lax.fori_loop(0, ITERS - 1, sweep, 0)
+
+    def next_copy(mu):
+        return pltpu.make_async_remote_copy(
+            src_ref=outgoing.at[mu - 1] if mu else state.at[0, :, pl.ds(0, 2)],
+            dst_ref=ahead.at[mu - 1] if mu else ahead_x,
+            send_sem=n_send.at[int(mu > 0)], recv_sem=n_recv.at[mu],
             device_id={"ta": lax.rem(a + c + n_ta - 1, n_ta), "gy": 1 - c},
             device_id_type=MESH_ID,
         )
-        for mu in range(3)
-    ]
 
     def send_next(mu):
-        for v in range(2):
-            for h in range(2):
-                blocks = [state[mu, :, 0:2, j, v, h] for j in range(3)]
-                for s in range(2):
-                    outgoing[mu, 2 * s + v, h] = side_by_side(
-                        blocks, lambda j: (window * j + width - seg * s) % width
-                    )
-        next_copies[mu].start()
+        if mu:
+            for ri in range(2):
+                for r in range(2):
+                    for j in range(3):
+                        rest = state[mu, ri, r, j, 2]
+                        for tile in range(2):
+                            full = state[mu, ri, r, j, tile]
+                            dense = turn(rest, 3 * quarter - HALO - slot * tile)
+                            for g in reversed(range(3)):
+                                dense = jnp.where(
+                                    lane < quarter * (g + 1),
+                                    turn(full, (quarter - slot) * g - HALO),
+                                    dense,
+                                )
+                            outgoing[mu - 1, ri, r, j, tile] = dense
+        next_copy(mu).start()
+
+    def later_links(mu, tile):
+        if mu == 0:
+            return closed(lambda ri, r, j: ahead_x[ri, r, j, tile])
+
+        def entry(ri, r, j):
+            if tile < 2:
+                dense = ahead[mu - 1, ri, r, j, tile]
+                return by_slot([turn(dense, (slot - quarter) * g + HALO) for g in range(3)])
+            return by_slot([
+                turn(ahead[mu - 1, ri, r, j, half], slot * half + HALO - 3 * quarter)
+                for half in range(2)
+            ])
+
+        return closed(entry)
     pl.semaphore_wait(side_sem, 1)
     staples(pairs[0:2])
     update((0,))
@@ -550,46 +586,59 @@
     arrived(2)
     unpack(3)
 
-    def time_firsts_at(index, carry):
-        v, h = index // 2, lax.rem(index, 2)
-        for nu in range(3):
-            u_nu = here(nu, v, h)
-            keep(ups, nu, v, h, times(u_nu, plus(3, nu, v, h), rows=2))
-            keep(lows, nu, v, h, times(u_nu, here(3, v, h), lhs_dag=True, rows=2))
-        return carry
-
-    def time_staples_at(nu, index, carry):
-        v, h = index // 2, lax.rem(index, 2)
-        later = spread(lambda z, hh, ri, r: ahead[nu, z, hh, ri, r], v, h)
-        up = get(lambda ri, r, j: ups[nu, ri, r, j, v, h], rows=2)
-        keep(ups, nu, v, h, times(up, later, rhs_dag=True, rows=2))
-        low = get(lambda ri, r, j: lows[nu, ri, r, j, v, h], rows=2)
-        keep(lows, nu, v, h, times(low, later, rows=2))
-        return carry
-
-    place = lax.rem(lane, seg)
-    inside = (place >= HALO) & (place < HALO + quarter)
-
-    def smooth(v, h, out_ref):
-        mat = mix(3, v, h, [(nu, nu) for nu in range(3)], smear_weight / 6.0)
+    def time_firsts():
+        for tile in tiles:
+            for nu in range(3):
+                u_nu = here(nu, tile)
+                keep(ups, nu, tile, times(u_nu, plus(3, nu, tile), rows=2))
+                keep(lows, nu, tile, times(u_nu, here(3, tile), lhs_dag=True, rows=2))
+
+    def time_staples(nu):
+        for tile in tiles:
+            later = later_links(nu, tile)
+            up = get(lambda ri, r, j: ups[nu, ri, r, j, tile], rows=2)
+            keep(ups, nu, tile, times(up, later, rhs_dag=True, rows=2))
+            low = get(lambda ri, r, j: lows[nu, ri, r, j, tile], rows=2)
+            keep(lows, nu, tile, times(low, later, rows=2))
+
+    def smooth(tile):
+        return mix(3, tile, [(nu, nu) for nu in range(3)], smear_weight / 6.0)
+
+    me = n_gy * a + c
+
+    def deliver(z, mats):
         for r in range(2):
             for j in range(3):
-                re, im = mat[r][j]
-                out_ref[r, j] = jnp.where(inside, re, pltpu.roll(im, quarter, 1))
-    lax.fori_loop(0, 4, time_firsts_at, 0)
+                dense = None
+                for p in reversed(range(4)):
+                    mat, g = mats[p // 2]
+                    piece = turn(mat[r][j][p % 2], quarter * p - slot * g - HALO)
+                    dense = (
+                        piece if dense is None
+                        else jnp.where(lane < quarter * (p + 1), piece, dense)
+                    )
+                smooth_out[z, r, j] = dense
+
+        @pl.when(me == z)
+        def _():
+            smooth_in[z] = smooth_out[z]
+
+        @pl.when(me != z)
+        def _():
+            pltpu.make_async_remote_copy(
+                src_ref=smooth_out.at[z], dst_ref=smooth_in.at[me],
+                send_sem=w_send.at[0], recv_sem=w_recv.at[0],
+                device_id={"ta": z // n_gy, "gy": z % n_gy}, device_id_type=MESH_ID,
+            ).start()
+    time_firsts()
     for nu in range(3):
-        next_copies[nu].wait_recv()
-        lax.fori_loop(0, 4, partial(time_staples_at, nu), 0)
-    for da, dc in ((1, 0), (1, 1), (0, 1)):
-        to_a, to_c = lax.rem(a + da, n_ta), lax.rem(c + dc, n_gy)
-        smooth(to_c, to_a, smooth_out.at[2 * da + dc])
-        copy = pltpu.make_async_remote_copy(
-            src_ref=smooth_out.at[2 * da + dc], dst_ref=smooth_in.at[n_gy * a + c],
-            send_sem=w_send.at[0], recv_sem=w_recv.at[0],
-            device_id={"ta": to_a, "gy": to_c}, device_id_type=MESH_ID,
-        )
-        copy.start()
-    smooth(c, a, smooth_in.at[n_gy * a + c])
+        next_copy(nu).wait_recv()
+        time_staples(nu)
+    last = smooth(2)
+    deliver(3, [(last, 0), (last, 1)])
+    even, odd = smooth(0), smooth(1)
+    for z in range(3):
+        deliver(z, [(even, z), (odd, z)])
     settle(smooth_out.at[pl.ds(1, n_ta * n_gy - 1)], w_recv.at[0])
 
     def time_link(t):
@@ -610,23 +659,18 @@
             im_terms += [(1, p_re * q_im), (1, p_im * q_re)]
     trace_re = signed_sum(re_terms) / 3.0
     trace_im = signed_sum(im_terms) / 3.0
-    trace_out[0] = trace_re
-    trace_out[1] = trace_im
-    sum_re = jnp.sum(jnp.where(inside, trace_re, 0.0), axis=0, keepdims=True)
-    sum_im = jnp.sum(jnp.where(inside, trace_im, 0.0), axis=0, keepdims=True)
-    both_re = sum_re + pltpu.roll(sum_re, seg, 1)
-    both_im = sum_im + pltpu.roll(sum_im, seg, 1)
-    sums = jnp.where(lane[0:1] < seg, both_re, both_im)
+    trace = jnp.where(lax.rem(lane, 2 * quarter) < quarter, trace_re, turn(trace_im, quarter))
+    trace_out[...] = trace
+    sums = jnp.sum(trace, axis=0, keepdims=True)
     row_out[0] = sums
-    keeps_one = (a == c) & (lax.rem(k, 2) == c)
-    for s in range(2):
-        for ta in range(n_ta):
-            z = 2 * s + c
-            is_self = (z == k) & (a == ta) & (a == c)
+    keeps_one = k == me
+    for ta in range(n_ta):
+        for gy in range(n_gy):
+            is_self = keeps_one & (a == ta) & (c == gy)
             remote = pltpu.make_async_remote_copy(
                 src_ref=trace_out, dst_ref=traces.at[k],
                 send_sem=t_send.at[0], recv_sem=t_recv.at[0],
-                device_id={"ta": ta, "gz": z, "gy": a}, device_id_type=MESH_ID,
+                device_id={"ta": ta, "gz": me, "gy": gy}, device_id_type=MESH_ID,
             )
             local = pltpu.make_async_copy(trace_out, traces.at[k], t_recv.at[0])
             pl.when(jnp.logical_not(is_self))(remote.start)
@@ -646,14 +690,14 @@
         copy.start()
 
     settle(traces, t_recv.at[0])
-    s_me = k // 2
     for ri in range(2):
-        out = None
-        for z in range(n_gz):
-            shift = lax.rem(quarter * z + 2 * width - seg * s_me - HALO, width)
-            piece = pltpu.roll(traces[z, ri], shift, 1)
-            out = piece if out is None else jnp.where(lane >= quarter * z, piece, out)
-        poly_ref[ri] = out
+        for h in range(2):
+            out = None
+            for z in reversed(range(n_gz)):
+                piece = turn(traces[z], quarter * (z - 2 * h - ri))
+                out = piece if out is None else jnp.where(lane < quarter * (z + 1), piece, out)
+            half = pltpu.roll(out, lax.rem(8 - 4 * c, 8), 0)
+            poly_ref[ri, pl.ds(h, 4, stride=2)] = half[0:4]
     total = sums
     settle(rows_in.at[pl.ds(1, n_group - 1)], r_recv.at[0])
     for step in range(1, n_group):
@@ -661,7 +705,8 @@
     total_ref[...] = total
     settle(packed.at[pl.ds(0, own)], a_send.at[0])
     settle(packed.at[own, 0], a_send.at[1])
-    settle(outgoing, n_send.at[0])
+    settle(ahead_x, n_send.at[0])
+    settle(outgoing, n_send.at[1])
     settle(smooth_out.at[pl.ds(1, n_ta * n_gy - 1)], w_send.at[0])
 
     @pl.when(keeps_one)
@@ -673,13 +718,13 @@
         settle(traces, t_send.at[0])
 
     settle(rows_in.at[pl.ds(1, n_group - 1)], r_send.at[0])
-def hand_over(sites, poly_in, total_in, poly_ref, mean_ref):
+def hand_over(quarter, sites, poly_in, total_in, poly_ref, mean_ref):
     poly_ref[...] = poly_in[...]
     total = total_in[...]
-    seg = total.shape[1] // 2
     place = lax.broadcasted_iota(jnp.int32, total.shape, 1)
-    mean_ref[0] = jnp.sum(jnp.where(place < seg, total, 0.0)) / sites
-    mean_ref[1] = jnp.sum(jnp.where(place >= seg, total, 0.0)) / sites
+    real = lax.rem(place, 2 * quarter) < quarter
+    mean_ref[0] = jnp.sum(jnp.where(real, total, 0.0)) / sites
+    mean_ref[1] = jnp.sum(jnp.where(real, 0.0, total)) / sites
 
 
 def fused_on_device(mesh_shape, spatial_links, time_links):
@@ -702,27 +747,28 @@
         scratch_shapes=[
             vm(4, 2, 3, 3, 2),
             vm(n_gz, 2, 4, 2, 2),
-            vm(n_gz, 2, 4, 2, 2),
-            vm(4, 2, 3, 3, 2, 2),
-            vm(6, 2, 2, 3, 2, 2),
-            vm(6, 2, 2, 3, 2, 2),
-            vm(3, n_gz, 2, 2, 2),
-            vm(3, n_gz, 2, 2, 2),
+            pltpu.VMEM((n_gz, 4, 2, 2, 2 * 8, width), jnp.float32),
+            vm(4, 2, 3, 3, 3),
+            vm(6, 2, 2, 3, 3),
+            vm(6, 2, 2, 3, 3),
+            vm(2, 2, 2, 3, 2),
+            vm(2, 2, 2, 3, 2),
+            vm(2, 2, 3, 3),
             vm(4, 2, 3),
             vm(4, 2, 3),
-            vm(2),
-            vm(n_gz, 2),
+            vm(),
+            vm(n_gz),
             pltpu.VMEM((1, 1, width), jnp.float32),
             pltpu.VMEM((n_group, 1, width), jnp.float32),
             dma((4,)),
-            dma((2,)), dma((3,)), dma((1,)), dma((3,)),
+            dma((2,)), dma((3,)), dma((2,)), dma((3,)),
             *[dma((1,))] * 6,
             *[pltpu.SemaphoreType.REGULAR] * 3,
         ],
         compiler_params=pltpu.CompilerParams(collective_id=0, has_side_effects=True),
     )(spatial, times_in)
     poly, mean = pl.pallas_call(
-        partial(hand_over, sites),
+        partial(hand_over, width // n_gz, sites),
         out_shape=(
             jax.ShapeDtypeStruct((2, 8, width), jnp.float32),
             jax.ShapeDtypeStruct((2,), jnp.float32),
@@ -743,7 +789,7 @@
     window = width // n_gz + 2 * HALO
     return (
         per == (2, 1, 8) and n_ta == 2 and n_gz == 4 and n_gy == 2
-        and width == 128 and ITERS >= 2 and 3 * window <= width and 2 * window <= width
+        and width == 128 and ITERS >= 2 and window <= width // 3
     )
 
 

time: 37.6 us -> 34.1 us (0.907)
  Pallas kernels: 36.8 us -> 33.3 us
    pallas_call x1, Pallas kernels: 36.1 us -> 32.6 us  [fused_on_device(): pl.pallas_call(partial(fused_kernel, (n_ta, n_gz, n_gy, width, sites)), o...]
where the time goes in v3:
time: 34.1 us; the launch traced here: 33.9 us
  Pallas kernels  33.3 us (98%)
  between operations  0.64 us (2%)
    pallas_call x1, Pallas kernels, fused_on_device(): pl.pallas_call(partial(fused_kernel, (n_ta, n_gz, n_gy, width, sites)), o...  32.6 us

profile of v3, /device:TPU:0, one launch (start us, length us, event | category | flops | bytes accessed | tf_op | source)
XLA Modules:
  0.0 33.9 jit_solution(17163524882576084905)
XLA Ops:
  0.6 32.6 %shard_map.41 = (f32[2,8,128]{2,1,0:T(8,128)S(1)}, f32[1,128]{1,0:T(1,128)S(1)}) custom-call(f32[3,2,3,3,2,8,128]{6,5,4,3,2,1,0:T(8,128)} %bitcast.5, f32[2,3,3,2,8,128]{5,4,3,2,1,0:T(8,128)} %bitcast.6), custom_call_target="tpu_custom_call" | custom-call | tf_op jit(solution)/shard_map/pallas_call | solution.py:739
  33.3 0.6 %shard_map.42 = (f32[2,8,128]{2,1,0:T(8,128)}, f32[2]{0:T(128)}) custom-call(f32[2,8,128]{2,1,0:T(8,128)S(1)} %get-tuple-element.6.poly_in, f32[1,128]{1,0:T(1,128)S(1)} %get-tuple-element.7.total_in), custom_call_target="tpu_custom_call" | custom-call | tf_op jit(solution)/shard_map/pallas_call | solution.py:770

commit v4 on v3

--- a/solution.py
+++ b/solution.py
@@ -272,7 +272,7 @@
 
 def fused_kernel(
     dims, sl_hbm, tl_hbm, poly_ref, total_ref,
-    raw, packed, landed, state, ups, lows, outgoing, ahead, ahead_x, smooth_out, smooth_in,
+    raw, packed, landed, state, ups, lows, outgoing, outgoing_x, ahead, ahead_x, smooth_out, smooth_in,
     trace_out, traces, row_out, rows_in,
     load_sem, a_send, a_recv, n_send, n_recv, w_send, w_recv,
     t_send, t_recv, r_send, r_recv, near_sem, far_sem, side_sem,
@@ -324,11 +324,12 @@
             tile = moved_block if j == 0 else jnp.where(wide >= slot * j, moved_block, tile)
         return tile.reshape(2, 2, 8, width)
 
-    dests = [mirrored(middle + 1), mirrored(2 - 2 * middle), mirrored(3), k]
-    own = len(dests) - 1
+    first_dests = [mirrored(middle + 1), mirrored(2 - 2 * middle), mirrored(3), k]
+    own = n_gz - 1
+    later_dests = [own - i - (own - i <= k).astype(jnp.int32) for i in range(own)] + [k]
 
     def pack(hop, d):
-        dest = dests[hop]
+        dest = (later_dests if d > 1 else first_dests)[hop]
         for t in range(2):
             blocks = [raw[d, :, 0:2, j, t] for j in range(3)]
             packed[hop, t, d] = side_by_side(
@@ -348,10 +349,10 @@
         return pltpu.make_async_remote_copy(
             src_ref=src, dst_ref=dst,
             send_sem=a_send.at[hop // own], recv_sem=a_recv.at[group],
-            device_id={"gz": dests[hop], "gy": t}, device_id_type=MESH_ID,
+            device_id={"gz": (later_dests if group else first_dests)[hop], "gy": t}, device_id_type=MESH_ID,
         )
 
-    hops = list(range(len(dests)))
+    hops = list(range(n_gz))
 
     def hand_out(group):
         members = groups[group]
@@ -533,9 +534,13 @@
         return carry
     lax.fori_loop(0, ITERS - 1, sweep, 0)
 
+    comps = [(ri, r, j) for ri in range(2) for r in range(2) for j in range(3)]
+    n_dense = 2 * len(comps)
+    in_slot = lax.rem(lane, slot)
+
     def next_copy(mu):
         return pltpu.make_async_remote_copy(
-            src_ref=outgoing.at[mu - 1] if mu else state.at[0, :, pl.ds(0, 2)],
+            src_ref=outgoing.at[mu - 1] if mu else outgoing_x,
             dst_ref=ahead.at[mu - 1] if mu else ahead_x,
             send_sem=n_send.at[int(mu > 0)], recv_sem=n_recv.at[mu],
             device_id={"ta": lax.rem(a + c + n_ta - 1, n_ta), "gy": 1 - c},
@@ -543,35 +548,45 @@
         )
 
     def send_next(mu):
-        if mu:
-            for ri in range(2):
-                for r in range(2):
-                    for j in range(3):
-                        rest = state[mu, ri, r, j, 2]
-                        for tile in range(2):
-                            full = state[mu, ri, r, j, tile]
-                            dense = turn(rest, 3 * quarter - HALO - slot * tile)
-                            for g in reversed(range(3)):
-                                dense = jnp.where(
-                                    lane < quarter * (g + 1),
-                                    turn(full, (quarter - slot) * g - HALO),
-                                    dense,
-                                )
-                            outgoing[mu - 1, ri, r, j, tile] = dense
+        out = outgoing.at[mu - 1] if mu else outgoing_x
+        for q, (ri, r, j) in enumerate(comps):
+            rest = state[mu, ri, r, j, 2]
+            for tile in range(2):
+                full = state[mu, ri, r, j, tile]
+                dense = turn(rest, 3 * quarter - HALO - slot * tile)
+                for g in reversed(range(3)):
+                    dense = jnp.where(
+                        lane < quarter * (g + 1),
+                        turn(full, (quarter - slot) * g - HALO),
+                        dense,
+                    )
+                out[2 * q + tile] = dense
+        if mu == 0:
+            for tile in tiles:
+                edge = None
+                for q, (ri, r, j) in enumerate(comps):
+                    piece = turn(state[mu, ri, r, j, tile], q + 1 - HALO)
+                    edge = piece if edge is None else jnp.where(in_slot == q, piece, edge)
+                out[n_dense + tile] = edge
         next_copy(mu).start()
 
     def later_links(mu, tile):
-        if mu == 0:
-            return closed(lambda ri, r, j: ahead_x[ri, r, j, tile])
+        source = ahead.at[mu - 1] if mu else ahead_x
 
         def entry(ri, r, j):
+            q = comps.index((ri, r, j))
             if tile < 2:
-                dense = ahead[mu - 1, ri, r, j, tile]
-                return by_slot([turn(dense, (slot - quarter) * g + HALO) for g in range(3)])
-            return by_slot([
-                turn(ahead[mu - 1, ri, r, j, half], slot * half + HALO - 3 * quarter)
-                for half in range(2)
-            ])
+                dense = source[2 * q + tile]
+                value = by_slot([turn(dense, (slot - quarter) * g + HALO) for g in range(3)])
+            else:
+                value = by_slot([
+                    turn(source[2 * q + half], slot * half + HALO - 3 * quarter)
+                    for half in range(2)
+                ])
+            if mu == 0:
+                edge = turn(source[n_dense + tile], HALO - 1 - q)
+                value = jnp.where(in_slot == HALO - 1, edge, value)
+            return value
 
         return closed(entry)
     pl.semaphore_wait(side_sem, 1)
@@ -606,7 +621,7 @@
 
     me = n_gy * a + c
 
-    def deliver(z, mats):
+    def lay_out(z, mats):
         for r in range(2):
             for j in range(3):
                 dense = None
@@ -619,6 +634,7 @@
                     )
                 smooth_out[z, r, j] = dense
 
+    def deliver(z):
         @pl.when(me == z)
         def _():
             smooth_in[z] = smooth_out[z]
@@ -634,11 +650,11 @@
     for nu in range(3):
         next_copy(nu).wait_recv()
         time_staples(nu)
-    last = smooth(2)
-    deliver(3, [(last, 0), (last, 1)])
-    even, odd = smooth(0), smooth(1)
-    for z in range(3):
-        deliver(z, [(even, z), (odd, z)])
+    mats = [smooth(tile) for tile in tiles]
+    for z in range(n_gz):
+        lay_out(z, [(mats[0], z), (mats[1], z)] if z < 3 else [(mats[2], 0), (mats[2], 1)])
+    for z in range(n_gz):
+        deliver(z)
     settle(smooth_out.at[pl.ds(1, n_ta * n_gy - 1)], w_recv.at[0])
 
     def time_link(t):
@@ -663,18 +679,6 @@
     trace_out[...] = trace
     sums = jnp.sum(trace, axis=0, keepdims=True)
     row_out[0] = sums
-    keeps_one = k == me
-    for ta in range(n_ta):
-        for gy in range(n_gy):
-            is_self = keeps_one & (a == ta) & (c == gy)
-            remote = pltpu.make_async_remote_copy(
-                src_ref=trace_out, dst_ref=traces.at[k],
-                send_sem=t_send.at[0], recv_sem=t_recv.at[0],
-                device_id={"ta": ta, "gz": me, "gy": gy}, device_id_type=MESH_ID,
-            )
-            local = pltpu.make_async_copy(trace_out, traces.at[k], t_recv.at[0])
-            pl.when(jnp.logical_not(is_self))(remote.start)
-            pl.when(is_self)(local.start)
     for step in range(1, n_group):
         da, dk, dc = step // (n_gz * n_gy), step // n_gy % n_gz, step % n_gy
         device = {
@@ -688,6 +692,18 @@
             device_id=device, device_id_type=MESH_ID,
         )
         copy.start()
+    keeps_one = k == me
+    for ta in range(n_ta):
+        for gy in range(n_gy):
+            is_self = keeps_one & (a == ta) & (c == gy)
+            remote = pltpu.make_async_remote_copy(
+                src_ref=trace_out, dst_ref=traces.at[k],
+                send_sem=t_send.at[0], recv_sem=t_recv.at[0],
+                device_id={"ta": ta, "gz": me, "gy": gy}, device_id_type=MESH_ID,
+            )
+            local = pltpu.make_async_copy(trace_out, traces.at[k], t_recv.at[0])
+            pl.when(jnp.logical_not(is_self))(remote.start)
+            pl.when(is_self)(local.start)
 
     settle(traces, t_recv.at[0])
     for ri in range(2):
@@ -751,9 +767,10 @@
             vm(4, 2, 3, 3, 3),
             vm(6, 2, 2, 3, 3),
             vm(6, 2, 2, 3, 3),
-            vm(2, 2, 2, 3, 2),
-            vm(2, 2, 2, 3, 2),
-            vm(2, 2, 3, 3),
+            vm(2, 24),
+            vm(27),
+            vm(2, 24),
+            vm(27),
             vm(4, 2, 3),
             vm(4, 2, 3),
             vm(),

time: 34.1 us -> 32.6 us (0.956)
  Pallas kernels: 33.3 us -> 31.8 us
    pallas_call x1, Pallas kernels: 32.6 us -> 31.2 us  [fused_on_device(): pl.pallas_call(partial(fused_kernel, (n_ta, n_gz, n_gy, width, sites)), o...]
where the time goes in v4:
time: 32.6 us; the launch traced here: 32.5 us
  Pallas kernels  31.8 us (98%)
  between operations  0.64 us (2%)
    pallas_call x1, Pallas kernels, fused_on_device(): pl.pallas_call(partial(fused_kernel, (n_ta, n_gz, n_gy, width, sites)), o...  31.2 us

profile of v4, /device:TPU:0, one launch (start us, length us, event | category | flops | bytes accessed | tf_op | source)
XLA Modules:
  0.0 32.5 jit_solution(16846667954216276532)
XLA Ops:
  0.6 31.2 %shard_map.41 = (f32[2,8,128]{2,1,0:T(8,128)S(1)}, f32[1,128]{1,0:T(1,128)S(1)}) custom-call(f32[3,2,3,3,2,8,128]{6,5,4,3,2,1,0:T(8,128)} %bitcast.5, f32[2,3,3,2,8,128]{5,4,3,2,1,0:T(8,128)} %bitcast.6), custom_call_target="tpu_custom_call" | custom-call | tf_op jit(solution)/shard_map/pallas_call | solution.py:755
  31.8 0.6 %shard_map.42 = (f32[2,8,128]{2,1,0:T(8,128)}, f32[2]{0:T(128)}) custom-call(f32[2,8,128]{2,1,0:T(8,128)S(1)} %get-tuple-element.6.poly_in, f32[1,128]{1,0:T(1,128)S(1)} %get-tuple-element.7.total_in), custom_call_target="tpu_custom_call" | custom-call | tf_op jit(solution)/shard_map/pallas_call | solution.py:787

commit v5 on v4

--- a/solution.py
+++ b/solution.py
@@ -272,7 +272,7 @@
 
 def fused_kernel(
     dims, sl_hbm, tl_hbm, poly_ref, total_ref,
-    raw, packed, landed, state, ups, lows, outgoing, outgoing_x, ahead, ahead_x, smooth_out, smooth_in,
+    raw, packed, landed, state, stash, ups, lows, outgoing, outgoing_x, ahead, ahead_x, smooth_out, smooth_in,
     trace_out, traces, row_out, rows_in,
     load_sem, a_send, a_recv, n_send, n_recv, w_send, w_recv,
     t_send, t_recv, r_send, r_recv, near_sem, far_sem, side_sem,
@@ -316,13 +316,18 @@
         pltpu.make_async_copy(ref, ref, sem).wait()
 
     wide = lax.broadcasted_iota(jnp.int32, (32, width), 1)
-
-    def side_by_side(blocks, shift_of):
+    reach = quarter + 2 * HALO - 2
+    spare = width - 3 * reach
+    spread_over = list(range(8)) + [8]
+    spilled = 11
+
+    def side_by_side(d, t, dest):
         tile = None
         for j in range(3):
-            moved_block = pltpu.roll(blocks[j].reshape(32, width), shift_of(j), 1)
-            tile = moved_block if j == 0 else jnp.where(wide >= slot * j, moved_block, tile)
-        return tile.reshape(2, 2, 8, width)
+            shift = lax.rem(reach * j + HALO - 1 + width - quarter * dest + width, width)
+            moved_block = pltpu.roll(raw[d, :, 0:2, j, t].reshape(32, width), shift, 1)
+            tile = moved_block if j == 0 else jnp.where(wide >= reach * j, moved_block, tile)
+        return tile.reshape(4, 8, width)
 
     first_dests = [mirrored(middle + 1), mirrored(2 - 2 * middle), mirrored(3), k]
     own = n_gz - 1
@@ -331,24 +336,39 @@
     def pack(hop, d):
         dest = (later_dests if d > 1 else first_dests)[hop]
         for t in range(2):
-            blocks = [raw[d, :, 0:2, j, t] for j in range(3)]
-            packed[hop, t, d] = side_by_side(
-                blocks,
-                lambda j: lax.rem(slot * j + HALO + width - quarter * dest + width, width),
-            )
+            block = side_by_side(d, t, dest)
+            if d < 2:
+                spill = side_by_side(2, t, dest)[3]
+                for n in range(4):
+                    at = spread_over.index(4 * d + n)
+                    packed[hop, t, 4 * d + n] = jnp.where(
+                        lane < 3 * reach, block[n], turn(spill, 3 * reach - spare * at)
+                    )
+            elif d == 2:
+                at = spread_over.index(4 * d)
+                packed[hop, t, 4 * d] = jnp.where(
+                    lane < 3 * reach, block[0], turn(block[3], 3 * reach - spare * at)
+                )
+                packed[hop, t, pl.ds(4 * d + 1, 2)] = block[1:3]
+            else:
+                packed[hop, t, pl.ds(4 * d, 4)] = block
+
+    def turn(value, lanes):
+        lanes = lanes % width
+        return pltpu.roll(value, lanes, 1) if lanes else value
 
     groups = ((0, 1), (2,), (3,))
+    parts = [pl.ds(0, 8), pl.ds(8, 3), pl.ds(12, 4)]
 
     def exchange(hop, t_rel, group):
         t = lax.rem(c + t_rel, 2)
-        part = pl.ds(groups[group][0], len(groups[group]))
-        src = packed.at[hop, t, part]
-        dst = landed.at[k, part, :, :, pl.ds(pl.multiple_of(8 * c, 8), 8)]
+        src = packed.at[hop, t, parts[group]]
+        dst = landed.at[k, parts[group], pl.ds(pl.multiple_of(8 * c, 8), 8)]
         if hop == own and t_rel == 0:
             return pltpu.make_async_copy(src, dst, a_recv.at[group])
         return pltpu.make_async_remote_copy(
             src_ref=src, dst_ref=dst,
-            send_sem=a_send.at[hop // own], recv_sem=a_recv.at[group],
+            send_sem=a_send.at[hop // own + 2 * (group // 2)], recv_sem=a_recv.at[group],
             device_id={"gz": (later_dests if group else first_dests)[hop], "gy": t}, device_id_type=MESH_ID,
         )
 
@@ -356,7 +376,7 @@
 
     def hand_out(group):
         members = groups[group]
-        for d in members:
+        for d in ((0, 1, 2), (), (3,))[group]:
             loads[d].wait()
         for d in members:
             pack(0, d)
@@ -394,12 +414,7 @@
     hand_out(1)
 
     def arrived(group):
-        part = pl.ds(groups[group][0], len(groups[group]))
-        settle(landed.at[:, part], a_recv.at[group])
-
-    def turn(value, lanes):
-        lanes = lanes % width
-        return pltpu.roll(value, lanes, 1) if lanes else value
+        settle(landed.at[:, parts[group]], a_recv.at[group])
 
     def by_slot(values):
         tile = values[-1]
@@ -414,12 +429,30 @@
         rows.append(third_row(rows[0], rows[1]))
         return rows
 
+    def gather_spill():
+        for z in range(n_gz):
+            for half in range(2):
+                rows = pl.ds(8 * half, 8)
+                tile = None
+                for at, n in reversed(list(enumerate(spread_over))):
+                    piece = turn(landed[z, n, rows], spare * at - 3 * reach)
+                    tile = (
+                        piece if tile is None
+                        else jnp.where(lane < spare * (at + 1), piece, tile)
+                    )
+                landed[z, spilled, rows] = tile
+
     def unpack(d):
+        if d == 2:
+            gather_spill()
         for tile in tiles:
 
             def entry(ri, r, j):
                 return by_slot([
-                    turn(landed[z, d, ri, r, pl.ds(h, 8, stride=2)], slot * (g - j))
+                    turn(
+                        landed[z, 4 * d + 2 * ri + r, pl.ds(h, 8, stride=2)],
+                        slot * g - reach * j + 1,
+                    )
                     for g, (z, h) in enumerate(places[tile])
                 ])
 
@@ -500,6 +533,34 @@
                 keep(lows, slot_of[nu, mu], tile, times(u_mu, two, lhs_dag=True, rows=2))
                 keep(ups, slot_of[mu, nu], tile, times(two, nu_ahead, rhs_dag=True, rows=2))
 
+    final_x = 4
+
+    def staples_first():
+        for tile in tiles:
+            for nu in (1, 2):
+                u_mu, u_nu = here(0, tile), here(nu, tile)
+                nu_ahead, mu_ahead = plus(nu, 0, tile), plus(0, nu, tile)
+                one = times(u_mu, nu_ahead)
+                two = times(u_nu, mu_ahead)
+                keep(lows, slot_of[0, nu], tile, times(u_nu, one, lhs_dag=True, rows=2))
+                keep(ups, slot_of[0, nu], tile, times(two, nu_ahead, rhs_dag=True, rows=2))
+                for row, line in enumerate(one[0:2] + two):
+                    for j in range(3):
+                        for ri in range(2):
+                            stash[nu - 1, row, ri, j, tile] = line[j][ri]
+
+    def staples_rest(nu):
+        for tile in tiles:
+            rows = [
+                [(stash[nu - 1, row, 0, j, tile], stash[nu - 1, row, 1, j, tile])
+                 for j in range(3)]
+                for row in range(5)
+            ]
+            one, two = rows[0:2], rows[2:5]
+            keep(lows, slot_of[nu, 0], tile, times(here(0, tile), two, lhs_dag=True, rows=2))
+            mu_ahead = plus(0, nu, tile)
+            keep(ups, slot_of[nu, 0], tile, times(one, mu_ahead, rhs_dag=True, rows=2))
+
     def mix(d, tile, entries, factor):
         def entry(ri, r, j):
             total = None
@@ -549,10 +610,11 @@
 
     def send_next(mu):
         out = outgoing.at[mu - 1] if mu else outgoing_x
+        done = mu or final_x
         for q, (ri, r, j) in enumerate(comps):
-            rest = state[mu, ri, r, j, 2]
+            rest = state[done, ri, r, j, 2]
             for tile in range(2):
-                full = state[mu, ri, r, j, tile]
+                full = state[done, ri, r, j, tile]
                 dense = turn(rest, 3 * quarter - HALO - slot * tile)
                 for g in reversed(range(3)):
                     dense = jnp.where(
@@ -565,7 +627,7 @@
             for tile in tiles:
                 edge = None
                 for q, (ri, r, j) in enumerate(comps):
-                    piece = turn(state[mu, ri, r, j, tile], q + 1 - HALO)
+                    piece = turn(state[done, ri, r, j, tile], q + 1 - HALO)
                     edge = piece if edge is None else jnp.where(in_slot == q, piece, edge)
                 out[n_dense + tile] = edge
         next_copy(mu).start()
@@ -590,12 +652,16 @@
 
         return closed(entry)
     pl.semaphore_wait(side_sem, 1)
-    staples(pairs[0:2])
-    update((0,))
+    staples_first()
+    for tile in tiles:
+        entries = [(slot_of[0, nu], nu) for nu in (1, 2)]
+        put(final_x, tile, mix(0, tile, entries, smear_weight / 4.0))
     send_next(0)
+    staples_rest(1)
     staples(pairs[2:3])
     update((1,))
     send_next(1)
+    staples_rest(2)
     update((2,))
     send_next(2)
     arrived(2)
@@ -604,7 +670,7 @@
     def time_firsts():
         for tile in tiles:
             for nu in range(3):
-                u_nu = here(nu, tile)
+                u_nu = here(nu or final_x, tile)
                 keep(ups, nu, tile, times(u_nu, plus(3, nu, tile), rows=2))
                 keep(lows, nu, tile, times(u_nu, here(3, tile), lhs_dag=True, rows=2))
 
@@ -616,8 +682,25 @@
             low = get(lambda ri, r, j: lows[nu, ri, r, j, tile], rows=2)
             keep(lows, nu, tile, times(low, later, rows=2))
 
+    factor = smear_weight / 6.0
+
+    def sum_two():
+        for tile in tiles:
+            for ri, r, j in comps:
+                total = None
+                for nu in range(2):
+                    low = shift_minus(lambda other: lows[nu, ri, r, j, other], nu, tile)
+                    part = ups[nu, ri, r, j, tile] + low
+                    total = part if total is None else total + part
+                kept = (1.0 - smear_weight) * state[3, ri, r, j, tile]
+                ups[3, ri, r, j, tile] = kept + factor * total
+
     def smooth(tile):
-        return mix(3, tile, [(nu, nu) for nu in range(3)], smear_weight / 6.0)
+        def entry(ri, r, j):
+            low = shift_minus(lambda other: lows[2, ri, r, j, other], 2, tile)
+            return ups[3, ri, r, j, tile] + factor * (ups[2, ri, r, j, tile] + low)
+
+        return project_rows(get(entry, rows=2))
 
     me = n_gy * a + c
 
@@ -650,6 +733,8 @@
     for nu in range(3):
         next_copy(nu).wait_recv()
         time_staples(nu)
+        if nu == 1:
+            sum_two()
     mats = [smooth(tile) for tile in tiles]
     for z in range(n_gz):
         lay_out(z, [(mats[0], z), (mats[1], z)] if z < 3 else [(mats[2], 0), (mats[2], 1)])
@@ -719,8 +804,9 @@
     for step in range(1, n_group):
         total = total + rows_in[step]
     total_ref[...] = total
-    settle(packed.at[pl.ds(0, own)], a_send.at[0])
-    settle(packed.at[own, 0], a_send.at[1])
+    for late, sent in enumerate((pl.ds(0, 11), parts[2])):
+        settle(packed.at[pl.ds(0, own), :, sent], a_send.at[2 * late])
+        settle(packed.at[own, 0, sent], a_send.at[2 * late + 1])
     settle(ahead_x, n_send.at[0])
     settle(outgoing, n_send.at[1])
     settle(smooth_out.at[pl.ds(1, n_ta * n_gy - 1)], w_send.at[0])
@@ -762,9 +848,10 @@
         out_specs=(pl.BlockSpec(memory_space=pltpu.VMEM),) * 2,
         scratch_shapes=[
             vm(4, 2, 3, 3, 2),
-            vm(n_gz, 2, 4, 2, 2),
-            pltpu.VMEM((n_gz, 4, 2, 2, 2 * 8, width), jnp.float32),
-            vm(4, 2, 3, 3, 3),
+            vm(n_gz, 2, 16),
+            pltpu.VMEM((n_gz, 16, 2 * 8, width), jnp.float32),
+            vm(5, 2, 3, 3, 3),
+            vm(2, 5, 2, 3, 3),
             vm(6, 2, 2, 3, 3),
             vm(6, 2, 2, 3, 3),
             vm(2, 24),
@@ -778,7 +865,7 @@
             pltpu.VMEM((1, 1, width), jnp.float32),
             pltpu.VMEM((n_group, 1, width), jnp.float32),
             dma((4,)),
-            dma((2,)), dma((3,)), dma((2,)), dma((3,)),
+            dma((4,)), dma((3,)), dma((2,)), dma((3,)),
             *[dma((1,))] * 6,
             *[pltpu.SemaphoreType.REGULAR] * 3,
         ],

time: 32.6 us -> 32.2 us (0.988)
  Pallas kernels: 31.8 us -> 31.4 us
    pallas_call x1, Pallas kernels: 31.2 us -> 30.8 us  [fused_on_device(): pl.pallas_call(partial(fused_kernel, (n_ta, n_gz, n_gy, width, sites)), o...]
where the time goes in v5:
time: 32.2 us; the launch traced here: 32 us
  Pallas kernels  31.4 us (98%)
  between operations  0.64 us (2%)
    pallas_call x1, Pallas kernels, fused_on_device(): pl.pallas_call(partial(fused_kernel, (n_ta, n_gz, n_gy, width, sites)), o...  30.8 us

profile of v5, /device:TPU:0, one launch (start us, length us, event | category | flops | bytes accessed | tf_op | source)
XLA Modules:
  0.0 32.0 jit_solution(7419311432739094938)
XLA Ops:
  0.6 30.8 %shard_map.41 = (f32[2,8,128]{2,1,0:T(8,128)S(1)}, f32[1,128]{1,0:T(1,128)S(1)}) custom-call(f32[3,2,3,3,2,8,128]{6,5,4,3,2,1,0:T(8,128)} %bitcast.5, f32[2,3,3,2,8,128]{5,4,3,2,1,0:T(8,128)} %bitcast.6), custom_call_target="tpu_custom_call" | custom-call | tf_op jit(solution)/shard_map/pallas_call | solution.py:841
  31.4 0.6 %shard_map.42 = (f32[2,8,128]{2,1,0:T(8,128)}, f32[2]{0:T(128)}) custom-call(f32[2,8,128]{2,1,0:T(8,128)S(1)} %get-tuple-element.6.poly_in, f32[1,128]{1,0:T(1,128)S(1)} %get-tuple-element.7.total_in), custom_call_target="tpu_custom_call" | custom-call | tf_op jit(solution)/shard_map/pallas_call | solution.py:874

commit v6 on v5

--- a/solution.py
+++ b/solution.py
@@ -376,7 +376,7 @@
 
     def hand_out(group):
         members = groups[group]
-        for d in ((0, 1, 2), (), (3,))[group]:
+        for d in ((0, 1, 2), ())[group]:
             loads[d].wait()
         for d in members:
             pack(0, d)
@@ -412,6 +412,14 @@
 
     hand_out(0)
     hand_out(1)
+    loads[3].wait()
+    for hop in hops:
+        pack(hop, 3)
+
+    def start_late():
+        for hop in hops:
+            for t_rel in range(2):
+                exchange(hop, t_rel, 2).start()
 
     def arrived(group):
         settle(landed.at[:, parts[group]], a_recv.at[group])
@@ -587,7 +595,7 @@
         @pl.when(index == 0)
         def _():
             arrived(1)
-            hand_out(2)
+            start_late()
             unpack(2)
 
         staples(pairs[1:3])
@@ -703,6 +711,7 @@
         return project_rows(get(entry, rows=2))
 
     me = n_gy * a + c
+    rank = (a * n_gz + k) * n_gy + c
 
     def lay_out(z, mats):
         for r in range(2):
@@ -718,17 +727,11 @@
                 smooth_out[z, r, j] = dense
 
     def deliver(z):
-        @pl.when(me == z)
-        def _():
-            smooth_in[z] = smooth_out[z]
-
-        @pl.when(me != z)
-        def _():
-            pltpu.make_async_remote_copy(
-                src_ref=smooth_out.at[z], dst_ref=smooth_in.at[me],
-                send_sem=w_send.at[0], recv_sem=w_recv.at[0],
-                device_id={"ta": z // n_gy, "gy": z % n_gy}, device_id_type=MESH_ID,
-            ).start()
+        pltpu.make_async_remote_copy(
+            src_ref=smooth_out.at[z], dst_ref=smooth_in.at[me],
+            send_sem=w_send.at[0], recv_sem=w_recv.at[0],
+            device_id={"ta": z // n_gy, "gy": lax.rem(z, n_gy)}, device_id_type=MESH_ID,
+        ).start()
     time_firsts()
     for nu in range(3):
         next_copy(nu).wait_recv()
@@ -738,8 +741,9 @@
     mats = [smooth(tile) for tile in tiles]
     for z in range(n_gz):
         lay_out(z, [(mats[0], z), (mats[1], z)] if z < 3 else [(mats[2], 0), (mats[2], 1)])
-    for z in range(n_gz):
+    for z in (n_gy * (1 - a), n_gy * (1 - a) + 1, n_gy * a + 1 - c):
         deliver(z)
+    smooth_in[me] = smooth_out[me]
     settle(smooth_out.at[pl.ds(1, n_ta * n_gy - 1)], w_recv.at[0])
 
     def time_link(t):
@@ -764,19 +768,20 @@
     trace_out[...] = trace
     sums = jnp.sum(trace, axis=0, keepdims=True)
     row_out[0] = sums
-    for step in range(1, n_group):
-        da, dk, dc = step // (n_gz * n_gy), step // n_gy % n_gz, step % n_gy
-        device = {
-            "ta": lax.rem(a + da, n_ta),
-            "gz": lax.rem(k + dk, n_gz),
-            "gy": lax.rem(c + dc, n_gy),
-        }
-        copy = pltpu.make_async_remote_copy(
-            src_ref=row_out, dst_ref=rows_in.at[pl.ds(step, 1)],
-            send_sem=r_send.at[0], recv_sem=r_recv.at[0],
-            device_id=device, device_id_type=MESH_ID,
-        )
-        copy.start()
+    for z in range(n_gz):
+        for da in range(n_ta):
+            for dc in range(n_gy):
+                copy = pltpu.make_async_remote_copy(
+                    src_ref=row_out, dst_ref=rows_in.at[pl.ds(rank, 1)],
+                    send_sem=r_send.at[0], recv_sem=r_recv.at[0],
+                    device_id={"ta": lax.rem(a + da, n_ta), "gz": z, "gy": lax.rem(c + dc, n_gy)},
+                    device_id_type=MESH_ID,
+                )
+                if da or dc:
+                    copy.start()
+                else:
+                    pl.when(k != z)(copy.start)
+    rows_in[pl.ds(rank, 1)] = row_out[...]
     keeps_one = k == me
     for ta in range(n_ta):
         for gy in range(n_gy):
@@ -799,8 +804,8 @@
                 out = piece if out is None else jnp.where(lane < quarter * (z + 1), piece, out)
             half = pltpu.roll(out, lax.rem(8 - 4 * c, 8), 0)
             poly_ref[ri, pl.ds(h, 4, stride=2)] = half[0:4]
-    total = sums
     settle(rows_in.at[pl.ds(1, n_group - 1)], r_recv.at[0])
+    total = rows_in[0]
     for step in range(1, n_group):
         total = total + rows_in[step]
     total_ref[...] = total

time: 32.2 us -> 31.8 us (0.988)
    pallas_call x1, Pallas kernels: 30.8 us -> 30.4 us  [fused_on_device(): pl.pallas_call(partial(fused_kernel, (n_ta, n_gz, n_gy, width, sites)), o...]
where the time goes in v6:
time: 31.8 us; the launch traced here: 31.7 us
  Pallas kernels  31.1 us (98%)
  between operations  0.64 us (2%)
    pallas_call x1, Pallas kernels, fused_on_device(): pl.pallas_call(partial(fused_kernel, (n_ta, n_gz, n_gy, width, sites)), o...  30.4 us
    pallas_call x1, Pallas kernels, fused_on_device(): pl.pallas_call(partial(hand_over, width // n_gz, sites), out_shape=(jax.S...  0.64 us

profile of v6, /device:TPU:0, one launch (start us, length us, event | category | flops | bytes accessed | tf_op | source)
XLA Modules:
  0.0 31.7 jit_solution(5174413255624040190)
XLA Ops:
  0.6 30.4 %shard_map.41 = (f32[2,8,128]{2,1,0:T(8,128)S(1)}, f32[1,128]{1,0:T(1,128)S(1)}) custom-call(f32[3,2,3,3,2,8,128]{6,5,4,3,2,1,0:T(8,128)} %bitcast.5, f32[2,3,3,2,8,128]{5,4,3,2,1,0:T(8,128)} %bitcast.6), custom_call_target="tpu_custom_call" | custom-call | tf_op jit(solution)/shard_map/pallas_call | solution.py:846
  31.1 0.6 %shard_map.42 = (f32[2,8,128]{2,1,0:T(8,128)}, f32[2]{0:T(128)}) custom-call(f32[2,8,128]{2,1,0:T(8,128)S(1)} %get-tuple-element.6.poly_in, f32[1,128]{1,0:T(1,128)S(1)} %get-tuple-element.7.total_in), custom_call_target="tpu_custom_call" | custom-call | tf_op jit(solution)/shard_map/pallas_call | solution.py:879

commit v7 on v6

--- a/solution.py
+++ b/solution.py
@@ -284,6 +284,11 @@
     a, k, c = lax.axis_index("ta"), lax.axis_index("gz"), lax.axis_index("gy")
     lane = lax.broadcasted_iota(jnp.int32, (8, width), 1)
     n_group = n_ta * n_gz * n_gy
+    loads = [pltpu.make_async_copy(sl_hbm.at[d], raw.at[d], load_sem.at[d]) for d in range(3)]
+    loads.append(pltpu.make_async_copy(tl_hbm, raw.at[3], load_sem.at[3]))
+    for copy in loads:
+        copy.start()
+
     middle = lax.rem((k + 1) // 2, 2)
     far_half = k // 2
 
@@ -307,11 +312,6 @@
     def _():
         for core in range(n_gy):
             greet({"gz": mirrored(0), "gy": core})
-
-    loads = [pltpu.make_async_copy(sl_hbm.at[d], raw.at[d], load_sem.at[d]) for d in range(3)]
-    loads.append(pltpu.make_async_copy(tl_hbm, raw.at[3], load_sem.at[3]))
-    for copy in loads:
-        copy.start()
     def settle(ref, sem):
         pltpu.make_async_copy(ref, ref, sem).wait()
 

time: 31.8 us -> 31.8 us (level)
  no operation moved by 1% of the time
where the time goes in v7:
time: 31.8 us; the launch traced here: 31.7 us
  Pallas kernels  31.1 us (98%)
  between operations  0.64 us (2%)
    pallas_call x1, Pallas kernels, fused_on_device(): pl.pallas_call(partial(fused_kernel, (n_ta, n_gz, n_gy, width, sites)), o...  30.4 us
    pallas_call x1, Pallas kernels, fused_on_device(): pl.pallas_call(partial(hand_over, width // n_gz, sites), out_shape=(jax.S...  0.64 us

profile of v7, /device:TPU:0, one launch (start us, length us, event | category | flops | bytes accessed | tf_op | source)
XLA Modules:
  0.0 31.7 jit_solution(7287859210548675958)
XLA Ops:
  0.6 30.4 %shard_map.41 = (f32[2,8,128]{2,1,0:T(8,128)S(1)}, f32[1,128]{1,0:T(1,128)S(1)}) custom-call(f32[3,2,3,3,2,8,128]{6,5,4,3,2,1,0:T(8,128)} %bitcast.5, f32[2,3,3,2,8,128]{5,4,3,2,1,0:T(8,128)} %bitcast.6), custom_call_target="tpu_custom_call" | custom-call | tf_op jit(solution)/shard_map/pallas_call | solution.py:846
  31.1 0.6 %shard_map.42 = (f32[2,8,128]{2,1,0:T(8,128)}, f32[2]{0:T(128)}) custom-call(f32[2,8,128]{2,1,0:T(8,128)S(1)} %get-tuple-element.6.poly_in, f32[1,128]{1,0:T(1,128)S(1)} %get-tuple-element.7.total_in), custom_call_target="tpu_custom_call" | custom-call | tf_op jit(solution)/shard_map/pallas_call | solution.py:879
